TPU v7x, 8 devices: a whole 2x2x1 slice. The times are simulated.
8 devices in a mesh: dp: 1 (over z), tp: 2 (over y), kvp: 4 (over x, core).
Axes of the slice: x: 2, y: 2, z: 1, core: 2. Of those that a mesh axis runs over, the one named last changes fastest.
Arguments:
- x_in: bfloat16 [32, 5120], P('dp')
- ctx_len: int32 [32], P('dp')
- g_attn: bfloat16 [5120], replicated
- g_mlp: bfloat16 [5120], replicated
- w_qkv: bfloat16 [5120, 7168], P(None, 'tp')
- w_o: bfloat16 [5120, 5120], P(('tp', 'kvp'))
- w_gate: bfloat16 [5120, 13824], P(None, ('tp', 'kvp'))
- w_up: bfloat16 [5120, 13824], P(None, ('tp', 'kvp'))
- w_down: bfloat16 [13824, 5120], P(('tp', 'kvp'))
- k_cache: bfloat16 [32, 1024, 8, 128], P('dp', 'kvp', 'tp')
- v_cache: bfloat16 [32, 1024, 8, 128], P('dp', 'kvp', 'tp')
Outputs:
- output 1: bfloat16 [32, 5120], P('dp')
- output 2: bfloat16 [32, 1024, 8, 128], P('dp', 'kvp', 'tp')
- output 3: bfloat16 [32, 1024, 8, 128], P('dp', 'kvp', 'tp')
All inputs are finite; a program needn't handle non-finite values.
Results may differ from a plain program's by a relative error of at most 0.00830868.
Values sent between devices are 32-bit elements.
A program may use at most 1 GiB of HBM per device.

v0:
```python
import jax
import jax.numpy as jnp
from jax import lax
from jax.sharding import PartitionSpec as P

ROPE_THETA = 500000.0
EPS = 1e-5
NEG_FILL = -1e30


def rms_norm(values, gain_vec):
    x_f32 = values.astype(jnp.float32)
    inv_rms = lax.rsqrt(jnp.mean(x_f32 * x_f32, axis=-1, keepdims=True) + EPS)
    return (x_f32 * inv_rms * gain_vec.astype(jnp.float32)).astype(jnp.bfloat16)


def rope_tables(ctx_len, head_dim):
    inv_freq = ROPE_THETA ** (-2.0 * jnp.arange(head_dim // 2, dtype=jnp.float32) / head_dim)
    angles = ctx_len.astype(jnp.float32)[:, None] * inv_freq[None, :]
    return jnp.cos(angles), jnp.sin(angles)


def rotary(vectors, cos_t, sin_t):
    half_dim = vectors.shape[-1] // 2
    first_half = vectors[..., :half_dim]
    second_half = vectors[..., half_dim:]
    return jnp.concatenate([first_half * cos_t - second_half * sin_t, second_half * cos_t + first_half * sin_t], axis=-1)


def mlp_part(hidden, g_mlp, w_gate, w_up, w_down):
    normed = rms_norm(hidden, g_mlp)
    gate_pre = jnp.dot(normed, w_gate, preferred_element_type=jnp.float32)
    up_proj = jnp.dot(normed, w_up, preferred_element_type=jnp.float32)
    act_out = (jax.nn.silu(gate_pre) * up_proj).astype(jnp.bfloat16)
    return jnp.dot(act_out, w_down, preferred_element_type=jnp.float32)


def local_attention(x_in, ctx_len, g_attn, w_qkv, k_cache, v_cache, kvp_index):
    batch_rows, block_len, kv_local, head_dim = k_cache.shape
    group_size = w_qkv.shape[1] // (kv_local * head_dim) - 2
    normed = rms_norm(x_in, g_attn)
    qkv_all = jnp.dot(normed, w_qkv, preferred_element_type=jnp.float32).reshape(batch_rows, kv_local, group_size + 2, head_dim)
    cos_t, sin_t = rope_tables(ctx_len, head_dim)
    queries = rotary(qkv_all[:, :, :group_size], cos_t[:, None, None, :], sin_t[:, None, None, :]).astype(jnp.bfloat16)
    key_new = rotary(qkv_all[:, :, group_size], cos_t[:, None, :], sin_t[:, None, :]).astype(jnp.bfloat16)
    val_new = qkv_all[:, :, group_size + 1].astype(jnp.bfloat16)
    positions = kvp_index * block_len + jnp.arange(block_len)
    hit_mask = (positions[None, :] == ctx_len[:, None])[:, :, None, None]
    k_out = jnp.where(hit_mask, key_new[:, None], k_cache)
    v_out = jnp.where(hit_mask, val_new[:, None], v_cache)
    scores = jnp.einsum("bgrd,btgd->bgrt", queries, k_out, preferred_element_type=jnp.float32) * head_dim ** -0.5
    valid = (positions[None, :] <= ctx_len[:, None])[:, None, None, :]
    scores = jnp.where(valid, scores, NEG_FILL)
    local_max = jnp.max(scores, axis=-1)
    prob_w = jnp.exp(scores - local_max[..., None])
    local_sum = jnp.sum(prob_w, axis=-1)
    local_acc = jnp.einsum("bgrt,btgd->bgrd", prob_w.astype(jnp.bfloat16), v_out, preferred_element_type=jnp.float32)
    return local_max, local_sum, local_acc, k_out, v_out


def solution(mesh):
    x_spec = P("dp", None)
    cache_spec = P("dp", "kvp", "tp", None)
    model_axes = ("tp", "kvp")

    def layer_step(x_in, ctx_len, g_attn, g_mlp, w_qkv, w_o, w_gate, w_up, w_down, k_cache, v_cache):
        kvp_index = lax.axis_index("kvp")
        local_max, local_sum, local_acc, k_out, v_out = local_attention(x_in, ctx_len, g_attn, w_qkv, k_cache, v_cache, kvp_index)
        batch_rows = local_acc.shape[0]
        attn_width = local_acc.shape[1] * local_acc.shape[2] * local_acc.shape[3]
        rows_own = w_o.shape[0]
        global_max = lax.pmax(local_max, "kvp")
        rescale = jnp.exp(local_max - global_max)
        denom_sum = lax.psum(local_sum * rescale, "kvp")
        acc_part = (local_acc * rescale[..., None]).reshape(batch_rows, attn_width)
        acc_own = lax.psum_scatter(acc_part, "kvp", scatter_dimension=1, tiled=True)
        denom_rows = jnp.broadcast_to(denom_sum[..., None], local_acc.shape).reshape(batch_rows, attn_width)
        denom_own = lax.dynamic_slice_in_dim(denom_rows, kvp_index * rows_own, rows_own, axis=1)
        attn_own = (acc_own / denom_own).astype(jnp.bfloat16)
        attn_sum = lax.psum(jnp.dot(attn_own, w_o, preferred_element_type=jnp.float32), model_axes)
        hidden = (x_in.astype(jnp.float32) + attn_sum).astype(jnp.bfloat16)
        mlp_sum = lax.psum(mlp_part(hidden, g_mlp, w_gate, w_up, w_down), model_axes)
        x_out = (hidden.astype(jnp.float32) + mlp_sum).astype(jnp.bfloat16)
        return x_out, k_out, v_out

    in_specs = (x_spec, P("dp"), P(None), P(None), P(None, "tp"), P(model_axes, None), P(None, model_axes), P(None, model_axes), P(model_axes, None), cache_spec, cache_spec)
    return jax.shard_map(layer_step, mesh=mesh, in_specs=in_specs, out_specs=(x_spec, cache_spec, cache_spec), check_vma=False)
```

profile of v0, /device:TPU:0, one launch (start us, length us, event | category | flops | bytes accessed | tf_op | source)
XLA Modules:
  0.0 209.2 jit_solution(3466682721970633638)
XLA Ops:
  7.2 0.0 reduce-scatter.2.cloned.1.call-start
  7.2 0.7 convert_element_type.53
  7.9 1.1 fusion.16
  9.1 0.0 copy-start.3
  9.1 14.9 %fusion.27 = f32[32,3584]{1,0:T(8,128)S(1)} fusion(bf16[5120,3584]{1,0:T(8,128)(2,1)} %param.15, bf16[32,5120]{1,0:T(8,128)(2,1)} %param.11, f32[5120]{0:T(1024)S(1)} %convert_element_type.53, f32[32]{0:T(128)S(1)} %add_rsqrt_fusion.1), kind=kOutput, calls=%fused_computation.32 | convolution fusion | flops 1175060480 | bytes 37507200 | tf_op jit(solution)/shard_map/dot_general | solution.py:42
  24.0 0.2 reshape.203
  24.2 0.1 slice.30
  24.3 0.1 slice.43
  24.4 0.0 copy-done.3
  24.4 0.1 broadcast_compare_fusion.1
  24.5 0.1 multiply_cosine_fusion
  24.6 0.2 subtract_convert_fusion
  24.9 0.1 subtract_convert_fusion.1
  25.0 0.1 pad_maximum_fusion
  25.1 13.7 %broadcast_select_fusion.1 = (bf16[32,256,4,128]{3,2,1,0:T(4,128)(2,1)S(1)}, bf16[32,256,4,128]{3,2,1,0:T(4,128)(2,1)}) fusion(bf16[32,256,4,128]{3,2,1,0:T(4,128)(2,1)} %param.20, pred[32,256]{1,0:T(8,128)(4,1)S(1)} %get-tuple-element.14, bf16[32,4,128]{2,1,0:T(4,128)(2,1)S(1)} %pad_maximum_fusion, bf16[32,256,4,128]{3,2,1,0:T(4,128)(2,1)} %param.21, ...), kind=kLoop, calls=%fused_computation.5 | loop fusion | flops 8388608 | bytes 33628160 | tf_op jit(solution)/shard_map/jit(_where)/select_n | solution.py:49
  38.8 0.0 copy-start
  38.9 3.4 %copy-done = bf16[32,256,4,128]{3,2,1,0:T(4,128)(2,1)} copy-done((bf16[32,256,4,128]{3,2,1,0:T(4,128)(2,1)}, bf16[32,256,4,128]{3,2,1,0:T(4,128)(2,1)S(1)}, u32[]{:S(2)}) %copy-start) | copy-done | bytes 8388632
  42.2 2.4 %fusion.50 = (f32[32,4,5]{2,1,0:T(4,128)S(1)}, f32[32,4,5,256]{3,2,1,0:T(8,128)S(1)}) fusion(bf16[32,256,4,128]{3,2,1,0:T(4,128)(2,1)S(1)} %get-tuple-element.11, bf16[32,4,5,64]{3,2,1,0:T(8,128)(2,1)S(1)} %get-tuple-element.8, bf16[32,4,5,64]{3,2,1,0:T(8,128)(2,1)S(1)} %get-tuple-element.7, pred[32,256]{1,0:T(8,128)(4,1)S(1)} %get-tuple-element.13), kind=kOutput, calls=%fused_computation.65 | convolution fusion | flops 42761600 | bytes 9218560 | tf_op jit(solution)/shard_map/bgrd,btgd->bgrt/dot_general | solution.py:51
  44.7 13.8 %pmax.7 = f32[32,4,5]{2,1,0:T(4,128)S(1)} all-reduce(f32[32,4,5]{2,1,0:T(4,128)S(1)} %get-tuple-element.17), channel_id=1, replica_groups=mesh['dp'=1,'tp'=2,'kvp'=4] {'kvp'}, use_global_device_ids=true, to_apply=%region_2.3 | all-reduce | flops 640 | bytes 5120 | tf_op jit(solution)/shard_map/pmax | solution.py:72
  58.5 0.5 fusion.14
  59.0 0.0 copy-start.2
  59.0 0.0 copy-start.1
  59.0 4.7 %fusion.11 = f32[32,4,5,128]{3,2,1,0:T(8,128)S(1)} fusion(bf16[32,256,4,128]{3,2,1,0:T(4,128)(2,1)} %get-tuple-element.12, f32[32,4,5,256]{3,2,1,0:T(8,128)S(1)} %get-tuple-element.18, f32[32,4,5]{2,1,0:T(4,128)S(1)} %get-tuple-element.17, f32[32,4,5]{2,1,0:T(4,128)S(1)} %bitcast.20), kind=kOutput, calls=%fused_computation.10 | convolution fusion | flops 42352640 | bytes 9376768 | tf_op jit(solution)/shard_map/bgrt,btgd->bgrd/dot_general | solution.py:57
  63.7 0.8 reshape.204
  64.6 0.0 reduce-scatter.2.cloned.1.call-update
  64.6 0.0 all-reduce.3.cloned.1.call-start
  64.6 10.7 %psum.21 = f32[32,4,5]{2,1,0:T(4,128)S(1)} all-reduce(f32[32,4,5]{2,1,0:T(4,128)S(1)} %bitcast.17), channel_id=1, replica_groups=mesh['dp'=1,'tp'=2,'kvp'=4] {'kvp'}, use_global_device_ids=true, to_apply=%region_5.6 | all-reduce | flops 640 | bytes 5120 | tf_op jit(solution)/shard_map/psum | solution.py:74
  75.4 0.2 broadcast_in_dim.43
  75.6 0.1 reshape.205
  75.7 3.9 %reduce-scatter.2.cloned.1.call-done = f32[32,640]{1,0:T(8,128)} async-done(((f32[32,2560]{1,0:T(8,128)}), f32[32,640]{1,0:T(8,128)}) %reduce-scatter.2.cloned.1.call-update) | async-done | bytes 81936 | tf_op jit(solution)/shard_map/reduce_scatter | solution.py:76
  79.5 5.0 %fusion.44 = f32[32,5120]{1,0:T(8,128)} fusion(bf16[640,5120]{1,0:T(8,128)(2,1)} %param.16, f32[32,640]{1,0:T(8,128)} %reduce-scatter.2.cloned.1.call-done, f32[32,2560]{1,0:T(8,128)S(1)} %reshape.205, s32[]{:T(128)S(6)} %select_n.17), kind=kOutput, calls=%fused_computation.50 | convolution fusion | flops 209756160 | bytes 7372804 | tf_op jit(solution)/shard_map/dot_general | solution.py:80
  84.5 0.0 all-reduce.3.cloned.1.call-update
  84.5 0.2 all-reduce.5.cloned.1.call-start
  84.8 0.0 copy-done.2
  84.8 43.6 %all-reduce.3.cloned.1.call-done = f32[32,5120]{1,0:T(8,128)} async-done(((f32[32,5120]{1,0:T(8,128)}), f32[32,5120]{1,0:T(8,128)}) %all-reduce.3.cloned.1.call-update) | async-done | bytes 655376 | tf_op jit(solution)/shard_map/psum | solution.py:80
  128.4 0.0 copy-done.1
  128.4 1.3 fusion.20
  129.7 11.2 %fusion.42 = f32[32,1728]{1,0:T(8,128)S(1)} fusion(bf16[5120,1728]{0,1:T(8,128)(2,1)} %param.17, bf16[32,5120]{1,0:T(8,128)(2,1)S(1)} %get-tuple-element.4, f32[5120]{0:T(1024)S(1)} %convert_element_type.61, f32[32]{0:T(128)S(1)} %add_rsqrt_fusion), kind=kOutput, calls=%fused_computation.44 | convolution fusion | flops 566886400 | bytes 18264192 | tf_op jit(solution)/shard_map/dot_general | solution.py:32
  140.9 16.7 %fusion.24 = f32[32,5120]{1,0:T(8,128)} fusion(bf16[1728,5120]{1,0:T(8,128)(2,1)} %param.19, bf16[5120,1728]{0,1:T(8,128)(2,1)} %param.18, f32[32,1728]{1,0:T(8,128)S(1)} %fusion.42, bf16[32,5120]{1,0:T(8,128)(2,1)S(1)} %get-tuple-element.4, f32[5120]{0:T(1024)S(1)} %convert_element_type.61, f32[32]{0:T(128)S(1)} %add_rsqrt_fusion), kind=kOutput, calls=%fused_computation.28 | convolution fusion | flops 1133449216 | bytes 36614272 | tf_op jit(solution)/shard_map/dot_general | solution.py:35
  157.6 0.0 all-reduce.5.cloned.1.call-update
  157.6 43.2 %all-reduce.5.cloned.1.call-done = f32[32,5120]{1,0:T(8,128)} async-done(((f32[32,5120]{1,0:T(8,128)}), f32[32,5120]{1,0:T(8,128)}) %all-reduce.5.cloned.1.call-update) | async-done | bytes 655376 | tf_op jit(solution)/shard_map/psum | solution.py:82
  200.8 1.9 fusion.23
  (9 shorter events, 0.1 us)
Async XLA Ops:
  7.2 72.4 %reduce-scatter.2.cloned.1.call-start = ((), (), s32[]{:S(2)}) async-start(), calls=%async_computation.1 | async-start | bytes 409600 | tf_op jit(solution)/shard_map/reduce_scatter | solution.py:76
  9.1 15.3 %copy-start.3 = (s32[32]{0:T(128)S(1)}, s32[32]{0:T(128)}, u32[]{:S(2)}) copy-start(s32[32]{0:T(128)} %param.12) | copy-start | bytes 388
  38.8 3.4 %copy-start = (bf16[32,256,4,128]{3,2,1,0:T(4,128)(2,1)}, bf16[32,256,4,128]{3,2,1,0:T(4,128)(2,1)S(1)}, u32[]{:S(2)}) copy-start(bf16[32,256,4,128]{3,2,1,0:T(4,128)(2,1)S(1)} %get-tuple-element.11) | copy-start | bytes 25165828
  59.0 25.8 %copy-start.2 = (bf16[5120]{0:T(1024)(128)(2,1)S(1)}, bf16[5120]{0:T(1024)(128)(2,1)}, u32[]{:S(2)}) copy-start(bf16[5120]{0:T(1024)(128)(2,1)} %param.14) | copy-start | bytes 30724
  59.0 69.4 %copy-start.1 = (bf16[32,5120]{1,0:T(8,128)(2,1)S(1)}, bf16[32,5120]{1,0:T(8,128)(2,1)}, u32[]{:S(2)}) copy-start(bf16[32,5120]{1,0:T(8,128)(2,1)} %param.11) | copy-start | bytes 983044
  64.6 63.8 %all-reduce.3.cloned.1.call-start = ((), (), s32[]{:S(2)}) async-start(), calls=%async_computation.2 | async-start | bytes 1310720 | tf_op jit(solution)/shard_map/psum | solution.py:80
  84.5 116.3 %all-reduce.5.cloned.1.call-start = ((), (), s32[]{:S(2)}) async-start(), calls=%async_computation.3 | async-start | bytes 1310720 | tf_op jit(solution)/shard_map/psum | solution.py:82
Sparse Core Ops, SparseCore 0:
  64.7 14.7 reduce-scatter.1
  84.6 43.7 all-reduce.2
  157.7 43.0 all-reduce.4
where the time goes:
time: 210 us; the launch traced here: 209 us
  waiting for transfers between devices  90.8 us (43%)
  matrix products  54.8 us (26%)
  blocking collectives  24.5 us (12%)
  other arithmetic  19.9 us (9%)
  between operations  13.9 us (7%)
  local copies, waits for them, and re-layouts  4.93 us (2%)
    psum x1, waiting for transfers between devices, layer_step(): lax.psum(jnp.dot(attn_own, w_o, preferred_element_type=jnp.float32), mode...  43.6 us
    psum x1, waiting for transfers between devices, layer_step(): lax.psum(mlp_part(hidden, g_mlp, w_gate, w_up, w_down), model_axes)  43.2 us
    dot_general x1, matrix products, mlp_part(): return jnp.dot(act_out, w_down, preferred_element_type=jnp.float32)  16.7 us
    dot_general x1, matrix products, local_attention(): jnp.dot(normed, w_qkv, preferred_element_type=jnp.float32)  14.9 us
    pmax x1, blocking collectives, layer_step(): global_max = lax.pmax(local_max, 'kvp')  13.8 us
    select_n x1, other arithmetic, local_attention(): k_out = jnp.where(hit_mask, key_new[:, None], k_cache)  13.7 us
    dot_general x1, matrix products, mlp_part(): gate_pre = jnp.dot(normed, w_gate, preferred_element_type=jnp.float32)  11.2 us
    psum x1, blocking collectives, layer_step(): denom_sum = lax.psum(local_sum * rescale, 'kvp')  10.7 us
  transfers between devices with their start and end apart: 3, of which 3 were waited for; matrix products, arithmetic and copies ran while one was open for 0% of the time, Pallas kernels for 0%

commit v1 on v0

v1 whole, which is shorter than its diff:
```python
import jax
import jax.numpy as jnp
from jax import lax
from jax.experimental import pallas as pl
from jax.experimental.pallas import tpu as pltpu
from jax.sharding import PartitionSpec as P

ROPE_THETA = 500000.0
EPS = 1e-5
NEG_FILL = -1e30
MESH = pl.DeviceIdType.MESH
F32 = jnp.float32
BF16 = jnp.bfloat16

D = 5120
HD = 128
B = 32
T = 256
KVL = 4
GRP = 5
ROWS = 24
QCOLS = (GRP + 2) * HD
FFL = 1728
VMEM_MAX = 67043328


def remote(src, dst, send, recv, dev):
    return pltpu.make_async_remote_copy(src_ref=src, dst_ref=dst, send_sem=send, recv_sem=recv, device_id=dev, device_id_type=MESH)


def enter(peers):
    barrier = pltpu.get_barrier_semaphore()
    for peer in peers:
        pl.semaphore_signal(barrier, inc=1, device_id=peer, device_id_type=MESH)
    pl.semaphore_wait(barrier, len(peers))


CHUNKS = ((0, 2), (2, 2), (4, 2), (6, 1))


def qkv_kernel(x_ref, g_ref, cos_ref, sin_ref, w_ref, q_ref, kn_ref, vn_ref, wbuf, u_ref, ex, w_sem, m_send, m_recv, x_send, x_recv, r_send, r_recv):
    j = lax.axis_index("kvp")
    mate = {"kvp": j + 1 - 2 * lax.rem(j, 2)}
    side = {"kvp": lax.rem(j + 2, 4)}

    def load(i):
        first, n = CHUNKS[i]
        cols = pl.ds(pl.multiple_of(j * QCOLS + first * HD, HD), n * HD)
        return pltpu.make_async_copy(w_ref.at[:, cols], wbuf.at[:, pl.ds(first * HD, n * HD)], w_sem.at[i])

    load(0).start()
    load(1).start()
    enter((mate, side))
    xf = x_ref[...].astype(F32)
    inv = lax.rsqrt(jnp.mean(xf * xf, axis=-1, keepdims=True) + EPS)
    u_ref[...] = (x_ref[...].astype(F32) * inv * g_ref[...].astype(F32)).astype(BF16)
    q_ref[...] = jnp.zeros_like(q_ref)

    def piece(slot, i):
        first, n = CHUNKS[i]
        return ex.at[slot, pl.ds(first, n)]

    def to_mate(i):
        return remote(piece(j, i), piece(j, i), m_send.at[i], m_recv.at[i], mate)

    def to_side(i):
        return remote(piece(j, i), piece(j, i), x_send.at[i], x_recv.at[i], side)

    def relay(i):
        slot = lax.rem(j + 2, 4)
        return remote(piece(slot, i), piece(slot, i), r_send.at[i], r_recv.at[i], mate)

    for i, (first, n) in enumerate(CHUNKS):
        load(i).wait()
        if i + 2 < len(CHUNKS):
            load(i + 2).start()
        res = jnp.dot(u_ref[...], wbuf[:, first * HD:(first + n) * HD], preferred_element_type=F32)
        for h in range(n):
            tile = res[:, h * HD:(h + 1) * HD]
            if first + h < GRP + 1:
                tile = tile * cos_ref[...] + pltpu.roll(tile, HD // 2, 1) * sin_ref[...]
            ex[j, first + h] = tile
        to_side(i).start()
        to_mate(i).start()
    for i in range(len(CHUNKS)):
        to_side(i).wait_recv()
        relay(i).start()
    for i in range(len(CHUNKS)):
        to_mate(i).wait_recv()
        relay(i).wait_recv()
    for g in range(KVL):
        for r in range(GRP):
            q_ref[pl.ds(g * GRP + r, B, stride=ROWS), :] = ex[g, r]
        kn = ex[g, GRP]
        vn = ex[g, GRP + 1]
        for half in range(2):
            kn_ref[pl.ds(half * KVL + g, B, stride=8), :] = kn
            vn_ref[pl.ds(half * KVL + g, B, stride=8), :] = vn
    for i in range(len(CHUNKS)):
        to_side(i).wait_send()
        to_mate(i).wait_send()
        relay(i).wait_send()


PAIRS = B // 2


def attn_kernel(ctx_ref, q_ref, kn_ref, vn_ref, k_ref, v_ref, part_ref, ko_ref, vo_ref, kbuf, vbuf, bias, acc2, m2, l2, in_sem, out_sem):
    base = lax.axis_index("kvp") * T

    def fetch(p, which):
        src, dst = ((k_ref, kbuf), (v_ref, vbuf))[which]
        return pltpu.make_async_copy(src.at[pl.ds(2 * p, 2)], dst.at[pl.ds(2 * p, 2)], in_sem.at[which, p])

    def flush(p, which):
        src, dst = ((kbuf, ko_ref), (vbuf, vo_ref))[which]
        return pltpu.make_async_copy(src.at[pl.ds(2 * p, 2)], dst.at[pl.ds(2 * p, 2)], out_sem.at[which, p])

    @pl.loop(0, PAIRS)
    def _(p):
        fetch(p, 0).start()
        fetch(p, 1).start()

    row = lax.broadcasted_iota(jnp.int32, (2 * ROWS, KVL * T), 0)
    row = jnp.where(row >= ROWS, row - ROWS, row)
    col = lax.broadcasted_iota(jnp.int32, (2 * ROWS, KVL * T), 1)
    head = (row >= GRP).astype(jnp.int32) + (row >= 2 * GRP).astype(jnp.int32) + (row >= 3 * GRP).astype(jnp.int32)
    bias[...] = jnp.where(head == (col & (KVL - 1)), 0.0, NEG_FILL)
    first_half = lax.broadcasted_iota(jnp.int32, (2 * ROWS, 1), 0) < ROWS
    wrow = lax.broadcasted_iota(jnp.int32, (16, HD), 0)

    def patch(b):
        pos = ctx_ref[b] - base

        @pl.when((pos >= 0) & (pos < T))
        def _():
            win = pl.ds(pl.multiple_of((pos // 4) * 16, 16), 16)
            hit = (wrow // KVL) == (pos & 3)
            for new_ref, buf in ((kn_ref, kbuf), (vn_ref, vbuf)):
                new8 = new_ref[pl.ds(b * 8, 8), :]
                new16 = jnp.concatenate([new8, new8], axis=0)
                buf[b, win, :] = jnp.where(hit, new16, buf[b, win, :].astype(F32)).astype(BF16)

    def attend(p):
        b = 2 * p
        q = q_ref[pl.ds(p * 2 * ROWS, 2 * ROWS), :]
        lhs = jnp.concatenate([jnp.where(first_half, q, 0.0), jnp.where(first_half, 0.0, q)], axis=1).astype(BF16)
        keys = jnp.concatenate([kbuf[b], kbuf[b + 1]], axis=1)
        s = lax.dot_general(lhs, keys, (((1,), (1,)), ((), ())), preferred_element_type=F32)
        lim = jnp.where(first_half, (ctx_ref[b] - base + 1) * KVL, (ctx_ref[b + 1] - base + 1) * KVL)
        cols = lax.broadcasted_iota(jnp.int32, (2 * ROWS, KVL * T), 1)
        s = jnp.where(cols < lim, s * HD ** -0.5 + bias[...], NEG_FILL)
        m = jnp.max(s, axis=1, keepdims=True)
        w = jnp.exp(s - m)
        values = jnp.concatenate([vbuf[b], vbuf[b + 1]], axis=1)
        o = jnp.dot(w.astype(BF16), values, preferred_element_type=F32)
        rows = pl.ds(p * 2 * ROWS, 2 * ROWS)
        acc2[rows, :] = jnp.where(first_half, o[:, :HD], o[:, HD:])
        m2[rows, :] = jnp.broadcast_to(m, (2 * ROWS, HD))
        l2[rows, :] = jnp.broadcast_to(jnp.sum(w, axis=1, keepdims=True), (2 * ROWS, HD))

    @pl.loop(0, PAIRS // 2)
    def _(it):
        for k in range(2):
            p = it * 2 + k
            fetch(p, 0).wait()
            fetch(p, 1).wait()
            patch(2 * p)
            patch(2 * p + 1)
            flush(p, 0).start()
            flush(p, 1).start()
        for k in range(2):
            attend(it * 2 + k)

    lane = lax.broadcasted_iota(jnp.int32, (B, HD), 1)
    for g in range(KVL):
        stats = jnp.zeros((B, HD), F32)
        for r in range(GRP):
            rows = pl.ds(g * GRP + r, B, stride=ROWS)
            part_ref[g, r] = acc2[rows, :]
            stats = jnp.where(lane == r, m2[rows, :], stats)
            stats = jnp.where(lane == 8 + r, l2[rows, :], stats)
        part_ref[g, GRP] = stats

    @pl.loop(0, PAIRS)
    def _(p):
        flush(p, 0).wait()
        flush(p, 1).wait()


NCH = 5
CW = D // NCH
GCH = 256


def tail_kernel(part_ref, x_ref, g_ref, wo_hbm, wg_hbm, wu_hbm, wd_hbm, out_ref,
                wo, wg, wu, wd, rx, attn, n_ref, y_ref, pbuf, sbuf, pair_a, pair_b, rs_a, rs_b, ag_a, ag_b,
                w_sem, gu_sem, wd_sem, c_send, c_recv, d_send, d_recv, s_send, s_recv, a_send, a_recv, f_send, f_recv):
    t = lax.axis_index("tp")
    j = lax.axis_index("kvp")
    core = lax.rem(j, 2)
    xpos = j // 2
    quarter = t * 2 + xpos
    mate = {"tp": t, "kvp": j + 1 - 2 * core}
    chips = []
    for e in (1, 2, 3):
        tt = t if e == 1 else 1 - t
        xx = xpos if e == 2 else 1 - xpos
        chips.append(({"tp": tt, "kvp": xx * 2 + core}, tt * 2 + xx))
    ring = [{"tp": t, "kvp": lax.rem(j + d, 4)} for d in (1, 2, 3)]

    wo_copy = pltpu.make_async_copy(wo_hbm, wo, w_sem)
    wo_copy.start()
    enter(tuple(ring) + (chips[1][0], chips[2][0]))

    def combine_copy(d):
        return remote(part_ref.at[lax.rem(j + d, 4)], rx.at[d - 1], c_send.at[d - 1], c_recv.at[d - 1], ring[d - 1])

    for d in (2, 1, 3):
        combine_copy(d).start()

    full = FFL // GCH
    rest = FFL - full * GCH
    spans = [(i * GCH, GCH) for i in range(full)] + [(full * GCH, rest)]

    def gate_copy(i, which):
        first, n = spans[i]
        src, dst = ((wg_hbm, wg), (wu_hbm, wu))[which]
        return pltpu.make_async_copy(src.at[pl.ds(first, n)], dst.at[pl.ds(first, n)], gu_sem.at[which, i])

    def down_copy(i):
        rows = pl.ds(i * (FFL // 4), FFL // 4)
        return pltpu.make_async_copy(wd_hbm.at[rows], wd.at[rows], wd_sem.at[i])

    wo_copy.wait()
    for i in range(len(spans)):
        gate_copy(i, 0).start()
        gate_copy(i, 1).start()
    for i in range(4):
        down_copy(i).start()

    for d in (1, 2, 3):
        combine_copy(d).wait_recv()
    stats = [part_ref[j, GRP]] + [rx[i, GRP] for i in range(3)]
    for r in range(GRP):
        ms = [s[:, r:r + 1] for s in stats]
        top = jnp.maximum(jnp.maximum(ms[0], ms[1]), jnp.maximum(ms[2], ms[3]))
        scales = [jnp.exp(m - top) for m in ms]
        denom = sum(sc * s[:, 8 + r:9 + r] for sc, s in zip(scales, stats))
        total = part_ref[j, r] * scales[0]
        for i in range(3):
            total = total + rx[i, r] * scales[i + 1]
        attn[:, r * HD:(r + 1) * HD] = (total / denom).astype(BF16)

    def all_sum(which, product, base, pair, rs, ag):
        def pair_copy(k):
            return remote(pbuf.at[k, pl.ds((1 - core) * 4, 4)], pair.at[k], d_send.at[which, k], d_recv.at[which, k], mate)

        def scatter_copy(k, e):
            dev, q = chips[e]
            return remote(sbuf.at[k, q], rs.at[k, e], s_send.at[which, k, e], s_recv.at[which, k, e], dev)

        own = core * 4 + quarter

        def gather_copy(k, e):
            dev = mate if e == 3 else chips[e][0]
            return remote(ag.at[k * 8 + own], ag.at[k * 8 + own], a_send.at[which, k, e], a_recv.at[which, k, e], dev)

        def forward_copy(k, e):
            slot = k * 8 + core * 4 + chips[e][1]
            return remote(ag.at[slot], ag.at[slot], f_send.at[which, k, e], f_recv.at[which, k, e], mate)

        for k in range(NCH):
            res = product(k)
            for i in range(8):
                pbuf[k, i] = res[:, i * HD:(i + 1) * HD]
            pair_copy(k).start()
        for k in range(NCH):
            pair_copy(k).wait_recv()
            for i in range(4):
                sbuf[k, i] = pbuf[k, core * 4 + i] + pair[k, i]
            for e in (2, 0, 1):
                scatter_copy(k, e).start()
        for k in range(NCH):
            for e in range(3):
                scatter_copy(k, e).wait_recv()
            total = sbuf[k, quarter] + rs[k, 0] + rs[k, 1] + rs[k, 2]
            ag[k * 8 + own] = (base(k * 8 + own) + total).astype(BF16).astype(F32)
            for e in (2, 0, 1, 3):
                gather_copy(k, e).start()
        for k in range(NCH):
            for e in range(3):
                gather_copy(k, e).wait_recv()
                forward_copy(k, e).start()
        for k in range(NCH):
            gather_copy(k, 3).wait_recv()
            for e in range(3):
                forward_copy(k, e).wait_recv()
        for k in range(NCH):
            pair_copy(k).wait_send()
            for e in range(3):
                scatter_copy(k, e).wait_send()
                forward_copy(k, e).wait_send()
            for e in range(4):
                gather_copy(k, e).wait_send()

    def o_product(k):
        return jnp.dot(attn[...], wo[:, k * CW:(k + 1) * CW], preferred_element_type=F32)

    def x_base(i):
        return x_ref[:, pl.ds(pl.multiple_of(i * HD, HD), HD)].astype(F32)

    all_sum(0, o_product, x_base, pair_a, rs_a, ag_a)

    squares = jnp.zeros((B, HD), F32)
    for i in range(D // HD):
        squares = squares + ag_a[i] * ag_a[i]
    inv = lax.rsqrt(jnp.sum(squares, axis=-1, keepdims=True) / D + EPS)
    for i in range(D // HD):
        cols = slice(i * HD, (i + 1) * HD)
        n_ref[:, cols] = (ag_a[i] * inv * g_ref[:, cols].astype(F32)).astype(BF16)

    def gate_step(first, n):
        dims = (((1,), (1,)), ((), ()))
        gate = lax.dot_general(n_ref[...], wg[pl.ds(first, n), :], dims, preferred_element_type=F32)
        up = lax.dot_general(n_ref[...], wu[pl.ds(first, n), :], dims, preferred_element_type=F32)
        return (jax.nn.silu(gate) * up).astype(BF16)

    for i, (first, n) in enumerate(spans):
        gate_copy(i, 0).wait()
        gate_copy(i, 1).wait()
        y_ref[:, first:first + n] = gate_step(first, n)
    for i in range(4):
        down_copy(i).wait()

    def down_product(k):
        return jnp.dot(y_ref[...], wd[:, k * CW:(k + 1) * CW], preferred_element_type=F32)

    all_sum(1, down_product, lambda i: ag_a[i], pair_b, rs_b, ag_b)
    for i in range(D // HD):
        out_ref[:, i * HD:(i + 1) * HD] = ag_b[i].astype(BF16)
    for d in (1, 2, 3):
        combine_copy(d).wait_send()


def vmem():
    return pl.BlockSpec(memory_space=pltpu.VMEM)


def hbm():
    return pl.BlockSpec(memory_space=pl.ANY)


def dma(*shape):
    return pltpu.SemaphoreType.DMA(shape)


def layer_step(x_in, ctx_len, g_attn, g_mlp, w_qkv, w_o, w_gate, w_up, w_down, k_cache, v_cache):
    inv_freq = ROPE_THETA ** (-2.0 * jnp.arange(HD // 2, dtype=F32) / HD)
    angles = ctx_len.astype(F32)[:, None] * inv_freq[None, :]
    cos_t, sin_t = jnp.cos(angles), jnp.sin(angles)
    cos_t = jnp.concatenate([cos_t, cos_t], axis=1)
    sin_t = jnp.concatenate([-sin_t, sin_t], axis=1)
    nch = len(CHUNKS)
    q2, kn, vn = pl.pallas_call(
        qkv_kernel,
        out_shape=(jax.ShapeDtypeStruct((B * ROWS, HD), F32), jax.ShapeDtypeStruct((B * 8, HD), F32), jax.ShapeDtypeStruct((B * 8, HD), F32)),
        in_specs=[vmem(), vmem(), vmem(), vmem(), hbm()],
        out_specs=(vmem(), vmem(), vmem()),
        scratch_shapes=[
            pltpu.VMEM((D, QCOLS), BF16), pltpu.VMEM((B, D), BF16), pltpu.VMEM((KVL, GRP + 2, B, HD), F32),
            dma(nch), dma(nch), dma(nch), dma(nch), dma(nch), dma(nch), dma(nch),
        ],
        compiler_params=pltpu.CompilerParams(collective_id=0, has_side_effects=True),
        name="qkv",
    )(x_in, g_attn.reshape(1, D), cos_t, sin_t, w_qkv)

    kc = k_cache.reshape(B, T * KVL, HD)
    vc = v_cache.reshape(B, T * KVL, HD)
    part, k_out, v_out = pl.pallas_call(
        attn_kernel,
        out_shape=(jax.ShapeDtypeStruct((KVL, GRP + 1, B, HD), F32), jax.ShapeDtypeStruct(kc.shape, BF16), jax.ShapeDtypeStruct(vc.shape, BF16)),
        in_specs=[pl.BlockSpec(memory_space=pltpu.SMEM), vmem(), vmem(), vmem(), hbm(), hbm()],
        out_specs=(vmem(), hbm(), hbm()),
        scratch_shapes=[
            pltpu.VMEM(kc.shape, BF16), pltpu.VMEM(vc.shape, BF16), pltpu.VMEM((2 * ROWS, KVL * T), F32),
            pltpu.VMEM((B * ROWS, HD), F32), pltpu.VMEM((B * ROWS, HD), F32), pltpu.VMEM((B * ROWS, HD), F32),
            dma(2, PAIRS), dma(2, PAIRS),
        ],
        name="attn",
    )(ctx_len, q2, kn, vn, kc, vc)

    x_out = pl.pallas_call(
        tail_kernel,
        out_shape=jax.ShapeDtypeStruct((B, D), BF16),
        in_specs=[vmem(), vmem(), vmem(), hbm(), hbm(), hbm(), hbm()],
        out_specs=vmem(),
        scratch_shapes=[
            pltpu.VMEM(w_o.shape, BF16), pltpu.VMEM((FFL, D), BF16), pltpu.VMEM((FFL, D), BF16), pltpu.VMEM((FFL, D), BF16),
            pltpu.VMEM((3, GRP + 1, B, HD), F32), pltpu.VMEM((B, GRP * HD), BF16), pltpu.VMEM((B, D), BF16), pltpu.VMEM((B, FFL), BF16),
            pltpu.VMEM((NCH, 8, B, HD), F32), pltpu.VMEM((NCH, 4, B, HD), F32),
            pltpu.VMEM((NCH, 4, B, HD), F32), pltpu.VMEM((NCH, 4, B, HD), F32),
            pltpu.VMEM((NCH, 3, B, HD), F32), pltpu.VMEM((NCH, 3, B, HD), F32),
            pltpu.VMEM((D // HD, B, HD), F32), pltpu.VMEM((D // HD, B, HD), F32),
            pltpu.SemaphoreType.DMA, dma(2, 7), dma(4), dma(3), dma(3),
            dma(2, NCH), dma(2, NCH), dma(2, NCH, 3), dma(2, NCH, 3), dma(2, NCH, 4), dma(2, NCH, 4), dma(2, NCH, 3), dma(2, NCH, 3),
        ],
        compiler_params=pltpu.CompilerParams(collective_id=1, has_side_effects=True, vmem_limit_bytes=VMEM_MAX),
        name="tail",
    )(part, x_in, g_mlp.reshape(1, D), w_o, w_gate.T, w_up.T, w_down)
    return x_out, k_out.reshape(k_cache.shape), v_out.reshape(v_cache.shape)


def solution(mesh):
    x_spec = P("dp", None)
    cache_spec = P("dp", "kvp", "tp", None)
    model_axes = ("tp", "kvp")
    in_specs = (x_spec, P("dp"), P(None), P(None), P(None, "tp"), P(model_axes, None), P(None, model_axes), P(None, model_axes), P(model_axes, None), cache_spec, cache_spec)
    return jax.shard_map(layer_step, mesh=mesh, in_specs=in_specs, out_specs=(x_spec, cache_spec, cache_spec), check_vma=False)
```

time: 210 us -> 83.2 us (0.40)
  waiting for transfers between devices: 90.8 us -> 0 us
  Pallas kernels: 0 us -> 77.1 us
  matrix products: 54.8 us -> 0 us
  blocking collectives: 24.5 us -> 0 us
  other arithmetic: 19.9 us -> 1.51 us
  between operations: 13.9 us -> 0.68 us
    psum x2 -> x0, waiting for transfers between devices: 86.8 us -> none  [the longest x1 43.6 us: layer_step(): lax.psum(jnp.dot(attn_own, w_o, preferred_element_type=jnp.float32), mode...]
    pallas_call x0 -> x3, Pallas kernels: none -> 77.1 us  [the longest x1 49.7 us: layer_step(): pl.pallas_call(tail_kernel, out_shape=jax.ShapeDtypeStruct((B, D), BF16),...]
    dot_general x6 -> x0, matrix products: 54.8 us -> none  [the longest x1 16.7 us: mlp_part(): return jnp.dot(act_out, w_down, preferred_element_type=jnp.float32)]
    pmax x1 -> x0, blocking collectives: 13.8 us -> none  [layer_step(): global_max = lax.pmax(local_max, 'kvp')]
    select_n x1 -> x0, other arithmetic: 13.7 us -> none  [local_attention(): k_out = jnp.where(hit_mask, key_new[:, None], k_cache)]
    psum x1 -> x0, blocking collectives: 10.7 us -> none  [layer_step(): denom_sum = lax.psum(local_sum * rescale, 'kvp')]
    reduce_scatter x1 -> x0, waiting for transfers between devices: 3.88 us -> none  [layer_step(): acc_own = lax.psum_scatter(acc_part, 'kvp', scatter_dimension=1, tiled=True)]
    reduce_sum x3 -> x0, other arithmetic: 2.9 us -> none  [the longest x2 2.43 us: rms_norm(): inv_rms = lax.rsqrt(jnp.mean(x_f32 * x_f32, axis=-1, keepdims=True) + EPS)]
  transfers between devices with their start and end apart: 3 -> 0, of which waited for: 3 -> 0; matrix products, arithmetic and copies ran while one was open for 0% -> 0% of each run, Pallas kernels for 0% -> 0%
where the time goes in v1:
time: 83.2 us; the launch traced here: 83 us
  Pallas kernels  77.1 us (93%)
  local copies, waits for them, and re-layouts  3.66 us (4%)
  other arithmetic  1.51 us (2%)
    pallas_call x1, Pallas kernels, layer_step(): pl.pallas_call(tail_kernel, out_shape=jax.ShapeDtypeStruct((B, D), BF16),...  49.7 us
    pallas_call x1, Pallas kernels, layer_step(): pl.pallas_call(attn_kernel, out_shape=(jax.ShapeDtypeStruct((KVL, GRP + 1...  14.5 us
    pallas_call x1, Pallas kernels, layer_step(): pl.pallas_call(qkv_kernel, out_shape=(jax.ShapeDtypeStruct((B * ROWS, HD)...  13 us
    unnamed x3, local copies, waits for them, and re-layouts  1.72 us

profile of v1, /device:TPU:0, one launch (start us, length us, event | category | flops | bytes accessed | tf_op | source)
XLA Modules:
  0.0 83.0 jit_solution(11413609577372596873)
XLA Ops:
  0.6 0.7 convert_element_type.3
  1.3 0.1 fusion
  1.5 0.7 pad_maximum_fusion
  2.1 1.3 %reshape.30.g_ref = bf16[1,5120]{1,0:T(2,128)(2,1)} reshape(bf16[5120]{0:T(1024)(128)(2,1)} %param.13) | data formatting | bytes 20480 | tf_op jit(solution)/shard_map/reshape | solution.py:376
  3.5 13.0 %qkv.1 = (f32[768,128]{1,0:T(8,128)}, f32[256,128]{1,0:T(8,128)}, f32[256,128]{1,0:T(8,128)}) custom-call(bf16[32,5120]{1,0:T(8,128)(2,1)} %x_ref.3, bf16[1,5120]{1,0:T(2,128)(2,1)} %reshape.30.g_ref, f32[32,128]{1,0:T(8,128)} %get-tuple-element.18.cos_ref, f32[32,128]{1,0:T(8,128)} %get-tuple-element.19.sin_ref, bf16[5120,3584]{1,0:T(8,128)(2,1)} %w_ref.1), custom_call_target="tpu_custom_call" | custom-call | tf_op jit(solution)/shard_map/qkv/pallas_call | solution.py:365
  16.5 0.0 copy-start
  16.5 14.5 %attn.1 = (f32[4,6,32,128]{3,2,1,0:T(8,128)}, bf16[32,1024,128]{2,1,0:T(8,128)(2,1)}, bf16[32,1024,128]{2,1,0:T(8,128)(2,1)}) custom-call(s32[32]{0:T(128)} %ctx_ref.1, f32[768,128]{1,0:T(8,128)} %get-tuple-element.9.q_ref, f32[256,128]{1,0:T(8,128)} %get-tuple-element.10.kn_ref, f32[256,128]{1,0:T(8,128)} %get-tuple-element.11.vn_ref, ...), custom_call_target="tpu_custom_call" | custom-call | tf_op jit(solution)/shard_map/attn/pallas_call | solution.py:380
  31.0 0.0 copy-done
  31.0 0.6 reshape.33.g_ref
  31.6 49.7 %tail.1 = bf16[32,5120]{1,0:T(8,128)(2,1)} custom-call(f32[4,6,32,128]{3,2,1,0:T(8,128)} %get-tuple-element.12.part_ref, bf16[32,5120]{1,0:T(8,128)(2,1)} %x_ref.3, bf16[1,5120]{1,0:T(2,128)(2,1)} %reshape.33.g_ref, bf16[640,5120]{1,0:T(8,128)(2,1)} %wo_hbm.1, bf16[1728,5120]{1,0:T(8,128)(2,1)} %bitcast.6, bf16[1728,5120]{1,0:T(8,128)(2,1)} %bitcast.7, ...), custom_call_target="tpu_custom_call" | custom-call | tf_op jit(solution)/shard_map/tail/pallas_call | solution.py:393
  81.3 1.7 %copy.15 = bf16[32,5120]{1,0:T(8,128)(2,1)} copy(bf16[32,5120]{1,0:T(8,128)(2,1)} %tail.1) | data formatting | bytes 655360
  (1 shorter events, 0.0 us)
Async XLA Ops:
  16.5 14.5 %copy-start = (bf16[5120]{0:T(1024)(128)(2,1)S(1)}, bf16[5120]{0:T(1024)(128)(2,1)}, u32[]{:S(2)}) copy-start(bf16[5120]{0:T(1024)(128)(2,1)} %param.14) | copy-start | bytes 30724

commit v2 on v1

--- a/solution.py
+++ b/solution.py
@@ -1,5 +1,6 @@
 import jax
 import jax.numpy as jnp
+import numpy as np
 from jax import lax
 from jax.experimental import pallas as pl
 from jax.experimental.pallas import tpu as pltpu
@@ -21,7 +22,8 @@
 ROWS = 24
 QCOLS = (GRP + 2) * HD
 FFL = 1728
-VMEM_MAX = 67043328
+MIB = 1024 * 1024
+TAIL_VMEM = 56 * MIB
 
 
 def remote(src, dst, send, recv, dev):
@@ -38,10 +40,20 @@
 CHUNKS = ((0, 2), (2, 2), (4, 2), (6, 1))
 
 
-def qkv_kernel(x_ref, g_ref, cos_ref, sin_ref, w_ref, q_ref, kn_ref, vn_ref, wbuf, u_ref, ex, w_sem, m_send, m_recv, x_send, x_recv, r_send, r_recv):
+def qkv_kernel(ctx_ref, freq_ref, x_hbm, g_hbm, w_ref, k_hbm, v_hbm, q_ref, kn_ref, vn_ref, kc_ref, vc_ref,
+               x_ref, g_ref, wbuf, u_ref, ex, x_sem, w_sem, c_sem, m_send, m_recv, x_send, x_recv, r_send, r_recv):
     j = lax.axis_index("kvp")
     mate = {"kvp": j + 1 - 2 * lax.rem(j, 2)}
     side = {"kvp": lax.rem(j + 2, 4)}
+    x_copy = pltpu.make_async_copy(x_hbm, x_ref, x_sem.at[0])
+    g_copy = pltpu.make_async_copy(g_hbm, g_ref, x_sem.at[1])
+    x_copy.start()
+    g_copy.start()
+
+    def cache_copy(i):
+        src, dst = ((k_hbm, kc_ref), (v_hbm, vc_ref))[i // 4]
+        some = pl.ds((i % 4) * 8, 8)
+        return pltpu.make_async_copy(src.at[some], dst.at[some], c_sem.at[i])
 
     def load(i):
         first, n = CHUNKS[i]
@@ -51,9 +63,25 @@
     load(0).start()
     load(1).start()
     enter((mate, side))
-    xf = x_ref[...].astype(F32)
-    inv = lax.rsqrt(jnp.mean(xf * xf, axis=-1, keepdims=True) + EPS)
-    u_ref[...] = (x_ref[...].astype(F32) * inv * g_ref[...].astype(F32)).astype(BF16)
+    row = lax.broadcasted_iota(jnp.int32, (B, HD), 0)
+    lane = lax.broadcasted_iota(jnp.int32, (B, HD), 1)
+    ctx = jnp.zeros((B, HD), F32)
+    for b in range(B):
+        ctx = jnp.where(row == b, ctx_ref[b].astype(F32), ctx)
+    angles = ctx * freq_ref[...]
+    cos_t = jnp.cos(angles)
+    sin_t = jnp.sin(angles)
+    sin_t = jnp.where(lane < HD // 2, -sin_t, sin_t)
+    x_copy.wait()
+    g_copy.wait()
+    squares = jnp.zeros((B, HD), F32)
+    for i in range(D // HD):
+        xf = x_ref[:, i * HD:(i + 1) * HD].astype(F32)
+        squares = squares + xf * xf
+    inv = lax.rsqrt(jnp.sum(squares, axis=-1, keepdims=True) / D + EPS)
+    for i in range(D // HD):
+        xf = x_ref[:, i * HD:(i + 1) * HD].astype(F32)
+        u_ref[:, i * HD:(i + 1) * HD] = (xf * inv * g_ref[i:i + 1, :].astype(F32)).astype(BF16)
     q_ref[...] = jnp.zeros_like(q_ref)
 
     def piece(slot, i):
@@ -74,11 +102,14 @@
         load(i).wait()
         if i + 2 < len(CHUNKS):
             load(i + 2).start()
+        else:
+            for c in range((i - 2) * 4, (i - 1) * 4):
+                cache_copy(c).start()
         res = jnp.dot(u_ref[...], wbuf[:, first * HD:(first + n) * HD], preferred_element_type=F32)
         for h in range(n):
             tile = res[:, h * HD:(h + 1) * HD]
             if first + h < GRP + 1:
-                tile = tile * cos_ref[...] + pltpu.roll(tile, HD // 2, 1) * sin_ref[...]
+                tile = tile * cos_t + pltpu.roll(tile, HD // 2, 1) * sin_t
             ex[j, first + h] = tile
         to_side(i).start()
         to_mate(i).start()
@@ -100,26 +131,20 @@
         to_side(i).wait_send()
         to_mate(i).wait_send()
         relay(i).wait_send()
+    for i in range(8):
+        cache_copy(i).wait()
 
 
 PAIRS = B // 2
 
 
-def attn_kernel(ctx_ref, q_ref, kn_ref, vn_ref, k_ref, v_ref, part_ref, ko_ref, vo_ref, kbuf, vbuf, bias, acc2, m2, l2, in_sem, out_sem):
+def attn_kernel(ctx_ref, q_ref, kn_ref, vn_ref, k_ref, v_ref, part_ref, kbuf, vbuf, ko_ref, vo_ref, bias, acc2, m2, l2, out_sem):
     base = lax.axis_index("kvp") * T
 
-    def fetch(p, which):
-        src, dst = ((k_ref, kbuf), (v_ref, vbuf))[which]
-        return pltpu.make_async_copy(src.at[pl.ds(2 * p, 2)], dst.at[pl.ds(2 * p, 2)], in_sem.at[which, p])
-
-    def flush(p, which):
+    def flush(i, which):
         src, dst = ((kbuf, ko_ref), (vbuf, vo_ref))[which]
-        return pltpu.make_async_copy(src.at[pl.ds(2 * p, 2)], dst.at[pl.ds(2 * p, 2)], out_sem.at[which, p])
-
-    @pl.loop(0, PAIRS)
-    def _(p):
-        fetch(p, 0).start()
-        fetch(p, 1).start()
+        some = pl.ds(4 * i, 4)
+        return pltpu.make_async_copy(src.at[some], dst.at[some], out_sem.at[which, i])
 
     row = lax.broadcasted_iota(jnp.int32, (2 * ROWS, KVL * T), 0)
     row = jnp.where(row >= ROWS, row - ROWS, row)
@@ -159,16 +184,15 @@
         m2[rows, :] = jnp.broadcast_to(m, (2 * ROWS, HD))
         l2[rows, :] = jnp.broadcast_to(jnp.sum(w, axis=1, keepdims=True), (2 * ROWS, HD))
 
+    @pl.loop(0, B // 4)
+    def _(it):
+        for k in range(4):
+            patch(it * 4 + k)
+        flush(it, 0).start()
+        flush(it, 1).start()
+
     @pl.loop(0, PAIRS // 2)
     def _(it):
-        for k in range(2):
-            p = it * 2 + k
-            fetch(p, 0).wait()
-            fetch(p, 1).wait()
-            patch(2 * p)
-            patch(2 * p + 1)
-            flush(p, 0).start()
-            flush(p, 1).start()
         for k in range(2):
             attend(it * 2 + k)
 
@@ -182,10 +206,10 @@
             stats = jnp.where(lane == 8 + r, l2[rows, :], stats)
         part_ref[g, GRP] = stats
 
-    @pl.loop(0, PAIRS)
-    def _(p):
-        flush(p, 0).wait()
-        flush(p, 1).wait()
+    @pl.loop(0, B // 4)
+    def _(i):
+        flush(i, 0).wait()
+        flush(i, 1).wait()
 
 
 NCH = 5
@@ -193,9 +217,9 @@
 GCH = 256
 
 
-def tail_kernel(part_ref, x_ref, g_ref, wo_hbm, wg_hbm, wu_hbm, wd_hbm, out_ref,
-                wo, wg, wu, wd, rx, attn, n_ref, y_ref, pbuf, sbuf, pair_a, pair_b, rs_a, rs_b, ag_a, ag_b,
-                w_sem, gu_sem, wd_sem, c_send, c_recv, d_send, d_recv, s_send, s_recv, a_send, a_recv, f_send, f_recv):
+def tail_kernel(part_ref, x_hbm, g_hbm, wo_hbm, wg_hbm, wu_hbm, wd_hbm, out_ref,
+                x_ref, g_ref, wo, wg, wu, rx, attn, n_ref, y_ref, pbuf, sbuf, pair_a, pair_b, rs_a, rs_b, ag_a, ag_b,
+                x_sem, w_sem, gu_sem, wd_sem, c_send, c_recv, d_send, d_recv, s_send, s_recv, a_send, a_recv, f_send, f_recv):
     t = lax.axis_index("tp")
     j = lax.axis_index("kvp")
     core = lax.rem(j, 2)
@@ -211,6 +235,10 @@
 
     wo_copy = pltpu.make_async_copy(wo_hbm, wo, w_sem)
     wo_copy.start()
+    x_copy = pltpu.make_async_copy(x_hbm, x_ref, x_sem.at[0])
+    g_copy = pltpu.make_async_copy(g_hbm, g_ref, x_sem.at[1])
+    x_copy.start()
+    g_copy.start()
     enter(tuple(ring) + (chips[1][0], chips[2][0]))
 
     def combine_copy(d):
@@ -229,15 +257,15 @@
         return pltpu.make_async_copy(src.at[pl.ds(first, n)], dst.at[pl.ds(first, n)], gu_sem.at[which, i])
 
     def down_copy(i):
-        rows = pl.ds(i * (FFL // 4), FFL // 4)
-        return pltpu.make_async_copy(wd_hbm.at[rows], wd.at[rows], wd_sem.at[i])
+        rows = pl.ds(*spans[i])
+        return pltpu.make_async_copy(wd_hbm.at[rows], wg.at[rows], wd_sem.at[i])
 
     wo_copy.wait()
+    x_copy.wait()
+    g_copy.wait()
     for i in range(len(spans)):
         gate_copy(i, 0).start()
         gate_copy(i, 1).start()
-    for i in range(4):
-        down_copy(i).start()
 
     for d in (1, 2, 3):
         combine_copy(d).wait_recv()
@@ -317,8 +345,7 @@
         squares = squares + ag_a[i] * ag_a[i]
     inv = lax.rsqrt(jnp.sum(squares, axis=-1, keepdims=True) / D + EPS)
     for i in range(D // HD):
-        cols = slice(i * HD, (i + 1) * HD)
-        n_ref[:, cols] = (ag_a[i] * inv * g_ref[:, cols].astype(F32)).astype(BF16)
+        n_ref[:, i * HD:(i + 1) * HD] = (ag_a[i] * inv * g_ref[i:i + 1, :].astype(F32)).astype(BF16)
 
     def gate_step(first, n):
         dims = (((1,), (1,)), ((), ()))
@@ -330,11 +357,12 @@
         gate_copy(i, 0).wait()
         gate_copy(i, 1).wait()
         y_ref[:, first:first + n] = gate_step(first, n)
-    for i in range(4):
+        down_copy(i).start()
+    for i in range(len(spans)):
         down_copy(i).wait()
 
     def down_product(k):
-        return jnp.dot(y_ref[...], wd[:, k * CW:(k + 1) * CW], preferred_element_type=F32)
+        return jnp.dot(y_ref[...], wg[:, k * CW:(k + 1) * CW], preferred_element_type=F32)
 
     all_sum(1, down_product, lambda i: ag_a[i], pair_b, rs_b, ag_b)
     for i in range(D // HD):
@@ -351,63 +379,78 @@
     return pl.BlockSpec(memory_space=pl.ANY)
 
 
+def in_hbm(a):
+    return pltpu.with_memory_space_constraint(a, pltpu.HBM)
+
+
+def in_vmem(a):
+    return pltpu.with_memory_space_constraint(a, pltpu.VMEM)
+
+
+def smem():
+    return pl.BlockSpec(memory_space=pltpu.SMEM)
+
+
 def dma(*shape):
     return pltpu.SemaphoreType.DMA(shape)
 
 
 def layer_step(x_in, ctx_len, g_attn, g_mlp, w_qkv, w_o, w_gate, w_up, w_down, k_cache, v_cache):
-    inv_freq = ROPE_THETA ** (-2.0 * jnp.arange(HD // 2, dtype=F32) / HD)
-    angles = ctx_len.astype(F32)[:, None] * inv_freq[None, :]
-    cos_t, sin_t = jnp.cos(angles), jnp.sin(angles)
-    cos_t = jnp.concatenate([cos_t, cos_t], axis=1)
-    sin_t = jnp.concatenate([-sin_t, sin_t], axis=1)
-    nch = len(CHUNKS)
-    q2, kn, vn = pl.pallas_call(
-        qkv_kernel,
-        out_shape=(jax.ShapeDtypeStruct((B * ROWS, HD), F32), jax.ShapeDtypeStruct((B * 8, HD), F32), jax.ShapeDtypeStruct((B * 8, HD), F32)),
-        in_specs=[vmem(), vmem(), vmem(), vmem(), hbm()],
-        out_specs=(vmem(), vmem(), vmem()),
-        scratch_shapes=[
-            pltpu.VMEM((D, QCOLS), BF16), pltpu.VMEM((B, D), BF16), pltpu.VMEM((KVL, GRP + 2, B, HD), F32),
-            dma(nch), dma(nch), dma(nch), dma(nch), dma(nch), dma(nch), dma(nch),
-        ],
-        compiler_params=pltpu.CompilerParams(collective_id=0, has_side_effects=True),
-        name="qkv",
-    )(x_in, g_attn.reshape(1, D), cos_t, sin_t, w_qkv)
-
+    freq = ROPE_THETA ** (-2.0 * np.arange(HD // 2, dtype=np.float64) / HD)
+    freq = np.concatenate([freq, freq]).astype(np.float32).reshape(1, HD)
     kc = k_cache.reshape(B, T * KVL, HD)
     vc = v_cache.reshape(B, T * KVL, HD)
-    part, k_out, v_out = pl.pallas_call(
+    nch = len(CHUNKS)
+    q2, kn, vn, kc, vc = pl.pallas_call(
+        qkv_kernel,
+        out_shape=(pltpu.VMEM((B * ROWS, HD), F32), pltpu.VMEM((B * 8, HD), F32), pltpu.VMEM((B * 8, HD), F32),
+                   pltpu.VMEM(kc.shape, BF16), pltpu.VMEM(vc.shape, BF16)),
+        in_specs=[smem(), vmem(), hbm(), hbm(), hbm(), hbm(), hbm()],
+        out_specs=(vmem(),) * 5,
+        scratch_shapes=[
+            pltpu.VMEM((B, D), BF16), pltpu.VMEM((D // HD, HD), BF16),
+            pltpu.VMEM((D, QCOLS), BF16), pltpu.VMEM((B, D), BF16), pltpu.VMEM((KVL, GRP + 2, B, HD), F32),
+            dma(2), dma(nch), dma(8), dma(nch), dma(nch), dma(nch), dma(nch), dma(nch), dma(nch),
+        ],
+        compiler_params=pltpu.CompilerParams(collective_id=0, has_side_effects=True, vmem_limit_bytes=MIB * 16),
+        name="qkv",
+    )(in_hbm(ctx_len), in_hbm(freq), in_hbm(x_in), in_hbm(g_attn.reshape(D // HD, HD)), in_hbm(w_qkv), in_hbm(kc), in_hbm(vc))
+
+    part, kc, vc, k_out, v_out = pl.pallas_call(
         attn_kernel,
-        out_shape=(jax.ShapeDtypeStruct((KVL, GRP + 1, B, HD), F32), jax.ShapeDtypeStruct(kc.shape, BF16), jax.ShapeDtypeStruct(vc.shape, BF16)),
-        in_specs=[pl.BlockSpec(memory_space=pltpu.SMEM), vmem(), vmem(), vmem(), hbm(), hbm()],
-        out_specs=(vmem(), hbm(), hbm()),
+        out_shape=(pltpu.VMEM((KVL, GRP + 1, B, HD), F32), pltpu.VMEM(kc.shape, BF16), pltpu.VMEM(vc.shape, BF16),
+                   jax.ShapeDtypeStruct(kc.shape, BF16), jax.ShapeDtypeStruct(vc.shape, BF16)),
+        in_specs=[smem(), vmem(), vmem(), vmem(), vmem(), vmem()],
+        out_specs=(vmem(), vmem(), vmem(), hbm(), hbm()),
         scratch_shapes=[
-            pltpu.VMEM(kc.shape, BF16), pltpu.VMEM(vc.shape, BF16), pltpu.VMEM((2 * ROWS, KVL * T), F32),
+            pltpu.VMEM((2 * ROWS, KVL * T), F32),
             pltpu.VMEM((B * ROWS, HD), F32), pltpu.VMEM((B * ROWS, HD), F32), pltpu.VMEM((B * ROWS, HD), F32),
-            dma(2, PAIRS), dma(2, PAIRS),
+            dma(2, B // 4),
         ],
+        input_output_aliases={4: 1, 5: 2},
+        compiler_params=pltpu.CompilerParams(vmem_limit_bytes=MIB * 4),
         name="attn",
-    )(ctx_len, q2, kn, vn, kc, vc)
+    )(in_hbm(ctx_len), q2, kn, vn, kc, vc)
 
     x_out = pl.pallas_call(
         tail_kernel,
-        out_shape=jax.ShapeDtypeStruct((B, D), BF16),
-        in_specs=[vmem(), vmem(), vmem(), hbm(), hbm(), hbm(), hbm()],
+        out_shape=pltpu.VMEM((B, D), BF16),
+        in_specs=[vmem(), hbm(), hbm(), hbm(), hbm(), hbm(), hbm()],
         out_specs=vmem(),
         scratch_shapes=[
-            pltpu.VMEM(w_o.shape, BF16), pltpu.VMEM((FFL, D), BF16), pltpu.VMEM((FFL, D), BF16), pltpu.VMEM((FFL, D), BF16),
+            pltpu.VMEM((B, D), BF16), pltpu.VMEM((D // HD, HD), BF16), pltpu.VMEM(w_o.shape, BF16), pltpu.VMEM((FFL, D), BF16), pltpu.VMEM((FFL, D), BF16),
             pltpu.VMEM((3, GRP + 1, B, HD), F32), pltpu.VMEM((B, GRP * HD), BF16), pltpu.VMEM((B, D), BF16), pltpu.VMEM((B, FFL), BF16),
             pltpu.VMEM((NCH, 8, B, HD), F32), pltpu.VMEM((NCH, 4, B, HD), F32),
             pltpu.VMEM((NCH, 4, B, HD), F32), pltpu.VMEM((NCH, 4, B, HD), F32),
             pltpu.VMEM((NCH, 3, B, HD), F32), pltpu.VMEM((NCH, 3, B, HD), F32),
             pltpu.VMEM((D // HD, B, HD), F32), pltpu.VMEM((D // HD, B, HD), F32),
-            pltpu.SemaphoreType.DMA, dma(2, 7), dma(4), dma(3), dma(3),
+            dma(2), pltpu.SemaphoreType.DMA, dma(2, 7), dma(7), dma(3), dma(3),
             dma(2, NCH), dma(2, NCH), dma(2, NCH, 3), dma(2, NCH, 3), dma(2, NCH, 4), dma(2, NCH, 4), dma(2, NCH, 3), dma(2, NCH, 3),
         ],
-        compiler_params=pltpu.CompilerParams(collective_id=1, has_side_effects=True, vmem_limit_bytes=VMEM_MAX),
+        compiler_params=pltpu.CompilerParams(collective_id=1, has_side_effects=True, vmem_limit_bytes=TAIL_VMEM),
+        cost_estimate=pl.CostEstimate(flops=10 ** 10, bytes_accessed=10 ** 8, transcendentals=0),
         name="tail",
-    )(part, x_in, g_mlp.reshape(1, D), w_o, w_gate.T, w_up.T, w_down)
+    )(in_vmem(part), in_hbm(x_in), in_hbm(g_mlp.reshape(D // HD, HD)), in_hbm(w_o), in_hbm(w_gate.T), in_hbm(w_up.T), in_hbm(w_down))
     return x_out, k_out.reshape(k_cache.shape), v_out.reshape(v_cache.shape)
 
 

time: 83.2 us -> 73 us (0.88)
  Pallas kernels: 77.1 us -> 71.5 us
  local copies, waits for them, and re-layouts: 3.66 us -> 0.73 us
  other arithmetic: 1.51 us -> 0 us
    pallas_call x3, Pallas kernels: 77.1 us -> 71.5 us  [the longest x1 49.4 us: layer_step(): pl.pallas_call(tail_kernel, out_shape=pltpu.VMEM((B, D), BF16), in_specs=...]
    reshape x2 -> x0, local copies, waits for them, and re-layouts: 1.94 us -> none  [the longest x1 1.32 us: layer_step(): g_attn.reshape(1, D)]
    unnamed x3 -> x1, local copies, waits for them, and re-layouts: 1.72 us -> 0.73 us
where the time goes in v2:
time: 73 us; the launch traced here: 72.9 us
  Pallas kernels  71.5 us (98%)
  local copies, waits for them, and re-layouts  0.73 us (1%)
    pallas_call x1, Pallas kernels, layer_step(): pl.pallas_call(tail_kernel, out_shape=pltpu.VMEM((B, D), BF16), in_specs=...  49.4 us
    pallas_call x1, Pallas kernels, layer_step(): pl.pallas_call(qkv_kernel, out_shape=(pltpu.VMEM((B * ROWS, HD), F32), pl...  12.5 us
    pallas_call x1, Pallas kernels, layer_step(): pl.pallas_call(attn_kernel, out_shape=(pltpu.VMEM((KVL, GRP + 1, B, HD),...  9.64 us

profile of v2, /device:TPU:0, one launch (start us, length us, event | category | flops | bytes accessed | tf_op | source)
XLA Modules:
  0.0 72.9 jit_solution(8565006002951545747)
XLA Ops:
  0.6 12.5 %qkv.1 = (f32[768,128]{1,0:T(8,128)S(1)}, f32[256,128]{1,0:T(8,128)S(1)}, f32[256,128]{1,0:T(8,128)S(1)}, bf16[32,1024,128]{2,1,0:T(8,128)(2,1)S(1)}, bf16[32,1024,128]{2,1,0:T(8,128)(2,1)S(1)}) custom-call(s32[32]{0:T(128)} %ctx_ref.3, f32[1,128]{1,0:T(1,128)} %constant.2.clone.freq_ref, bf16[32,5120]{1,0:T(8,128)(2,1)} %x_hbm.3, bf16[40,128]{1,0:T(8,128)(2,1)} %bitcast.13, ...), custom_call_target="tpu_custom_call" | custom-call | tf_op jit(solution)/shard_map/qkv/pallas_call | solution.py:404
  13.1 9.6 %attn.1 = (f32[4,6,32,128]{3,2,1,0:T(8,128)S(1)}, bf16[32,1024,128]{2,1,0:T(8,128)(2,1)S(1)}, bf16[32,1024,128]{2,1,0:T(8,128)(2,1)S(1)}, bf16[32,1024,128]{2,1,0:T(8,128)(2,1)}, bf16[32,1024,128]{2,1,0:T(8,128)(2,1)}) custom-call(s32[32]{0:T(128)} %ctx_ref.3, f32[768,128]{1,0:T(8,128)S(1)} %get-tuple-element.11.q_ref, ...), custom_call_target="tpu_custom_call", output_to_operand_aliasing={{1}: (4, {}), {2}: (5, {})} | custom-call | tf_op jit(solution)/shard_map/attn/pallas_call | solution.py:419
  22.8 49.4 %tail.1 = bf16[32,5120]{1,0:T(8,128)(2,1)S(1)} custom-call(f32[4,6,32,128]{3,2,1,0:T(8,128)S(1)} %get-tuple-element.16.part_ref, bf16[32,5120]{1,0:T(8,128)(2,1)} %x_hbm.3, bf16[40,128]{1,0:T(8,128)(2,1)} %bitcast.12, bf16[640,5120]{1,0:T(8,128)(2,1)} %wo_hbm.1, bf16[1728,5120]{1,0:T(8,128)(2,1)} %bitcast.8, bf16[1728,5120]{1,0:T(8,128)(2,1)} %bitcast.9, ...), custom_call_target="tpu_custom_call" | custom-call | flops 10000000000 | bytes 100000000 | tf_op jit(solution)/shard_map/tail/pallas_call | solution.py:435
  72.1 0.7 copy.20

commit v3 on v2

--- a/solution.py
+++ b/solution.py
@@ -215,10 +215,12 @@
 NCH = 5
 CW = D // NCH
 GCH = 256
+FLIP = 4
+FLIPS = (4, 1, 3, 3, 1)
 
 
 def tail_kernel(part_ref, x_hbm, g_hbm, wo_hbm, wg_hbm, wu_hbm, wd_hbm, out_ref,
-                x_ref, g_ref, wo, wg, wu, rx, attn, n_ref, y_ref, pbuf, sbuf, pair_a, pair_b, rs_a, rs_b, ag_a, ag_b,
+                x_ref, g_ref, wo, w2, rx, attn, n_ref, y_ref, pbuf, sbuf, pair_a, pair_b, rs_a, rs_b, ag_a, ag_b,
                 x_sem, w_sem, gu_sem, wd_sem, c_send, c_recv, d_send, d_recv, s_send, s_recv, a_send, a_recv, f_send, f_recv):
     t = lax.axis_index("tp")
     j = lax.axis_index("kvp")
@@ -253,12 +255,12 @@
 
     def gate_copy(i, which):
         first, n = spans[i]
-        src, dst = ((wg_hbm, wg), (wu_hbm, wu))[which]
-        return pltpu.make_async_copy(src.at[pl.ds(first, n)], dst.at[pl.ds(first, n)], gu_sem.at[which, i])
+        src = (wg_hbm, wu_hbm)[which]
+        return pltpu.make_async_copy(src.at[pl.ds(first, n)], w2.at[which, pl.ds(first, n)], gu_sem.at[which, i])
 
     def down_copy(i):
         rows = pl.ds(*spans[i])
-        return pltpu.make_async_copy(wd_hbm.at[rows], wg.at[rows], wd_sem.at[i])
+        return pltpu.make_async_copy(wd_hbm.at[rows], w2.at[0, rows], wd_sem.at[i])
 
     wo_copy.wait()
     x_copy.wait()
@@ -267,6 +269,22 @@
         gate_copy(i, 0).start()
         gate_copy(i, 1).start()
 
+    flipped = [0]
+
+    def flip(blocks):
+        for block in range(flipped[0], min(flipped[0] + blocks, 2 * full)):
+            i, which = block // 2, block % 2
+            gate_copy(i, which).wait()
+
+            @pl.loop(0, D // (GCH * FLIP))
+            def _(u):
+                for v in range(FLIP):
+                    rows = pl.ds(i * GCH, GCH)
+                    cols = pl.ds(pl.multiple_of((u * FLIP + v) * GCH, GCH), GCH)
+                    w2[which, rows, cols] = w2[which, rows, cols].T
+        flipped[0] += blocks
+
+    flip(FLIPS[0])
     for d in (1, 2, 3):
         combine_copy(d).wait_recv()
     stats = [part_ref[j, GRP]] + [rx[i, GRP] for i in range(3)]
@@ -303,12 +321,16 @@
             for i in range(8):
                 pbuf[k, i] = res[:, i * HD:(i + 1) * HD]
             pair_copy(k).start()
+        if which == 0:
+            flip(FLIPS[1])
         for k in range(NCH):
             pair_copy(k).wait_recv()
             for i in range(4):
                 sbuf[k, i] = pbuf[k, core * 4 + i] + pair[k, i]
             for e in (2, 0, 1):
                 scatter_copy(k, e).start()
+        if which == 0:
+            flip(FLIPS[2])
         for k in range(NCH):
             for e in range(3):
                 scatter_copy(k, e).wait_recv()
@@ -316,10 +338,14 @@
             ag[k * 8 + own] = (base(k * 8 + own) + total).astype(BF16).astype(F32)
             for e in (2, 0, 1, 3):
                 gather_copy(k, e).start()
+        if which == 0:
+            flip(FLIPS[3])
         for k in range(NCH):
             for e in range(3):
                 gather_copy(k, e).wait_recv()
                 forward_copy(k, e).start()
+        if which == 0:
+            flip(FLIPS[4])
         for k in range(NCH):
             gather_copy(k, 3).wait_recv()
             for e in range(3):
@@ -347,22 +373,33 @@
     for i in range(D // HD):
         n_ref[:, i * HD:(i + 1) * HD] = (ag_a[i] * inv * g_ref[i:i + 1, :].astype(F32)).astype(BF16)
 
-    def gate_step(first, n):
-        dims = (((1,), (1,)), ((), ()))
-        gate = lax.dot_general(n_ref[...], wg[pl.ds(first, n), :], dims, preferred_element_type=F32)
-        up = lax.dot_general(n_ref[...], wu[pl.ds(first, n), :], dims, preferred_element_type=F32)
+    def act(gate, up):
         return (jax.nn.silu(gate) * up).astype(BF16)
 
-    for i, (first, n) in enumerate(spans):
-        gate_copy(i, 0).wait()
-        gate_copy(i, 1).wait()
-        y_ref[:, first:first + n] = gate_step(first, n)
+    for i in range(full):
+        rows = pl.ds(i * GCH, GCH)
+        gate = up = None
+        for k in range(D // GCH):
+            cols = slice(k * GCH, (k + 1) * GCH)
+            g_k = jnp.dot(n_ref[:, cols], w2[0, rows, cols], preferred_element_type=F32)
+            u_k = jnp.dot(n_ref[:, cols], w2[1, rows, cols], preferred_element_type=F32)
+            gate = g_k if gate is None else gate + g_k
+            up = u_k if up is None else up + u_k
+        y_ref[:, i * GCH:(i + 1) * GCH] = act(gate, up)
         down_copy(i).start()
+    first, n = spans[full]
+    gate_copy(full, 0).wait()
+    gate_copy(full, 1).wait()
+    dims = (((1,), (1,)), ((), ()))
+    gate = lax.dot_general(n_ref[...], w2[0, pl.ds(first, n), :], dims, preferred_element_type=F32)
+    up = lax.dot_general(n_ref[...], w2[1, pl.ds(first, n), :], dims, preferred_element_type=F32)
+    y_ref[:, first:first + n] = act(gate, up)
+    down_copy(full).start()
     for i in range(len(spans)):
         down_copy(i).wait()
 
     def down_product(k):
-        return jnp.dot(y_ref[...], wg[:, k * CW:(k + 1) * CW], preferred_element_type=F32)
+        return jnp.dot(y_ref[...], w2[0, :, k * CW:(k + 1) * CW], preferred_element_type=F32)
 
     all_sum(1, down_product, lambda i: ag_a[i], pair_b, rs_b, ag_b)
     for i in range(D // HD):
@@ -438,7 +475,7 @@
         in_specs=[vmem(), hbm(), hbm(), hbm(), hbm(), hbm(), hbm()],
         out_specs=vmem(),
         scratch_shapes=[
-            pltpu.VMEM((B, D), BF16), pltpu.VMEM((D // HD, HD), BF16), pltpu.VMEM(w_o.shape, BF16), pltpu.VMEM((FFL, D), BF16), pltpu.VMEM((FFL, D), BF16),
+            pltpu.VMEM((B, D), BF16), pltpu.VMEM((D // HD, HD), BF16), pltpu.VMEM(w_o.shape, BF16), pltpu.VMEM((2, FFL, D), BF16),
             pltpu.VMEM((3, GRP + 1, B, HD), F32), pltpu.VMEM((B, GRP * HD), BF16), pltpu.VMEM((B, D), BF16), pltpu.VMEM((B, FFL), BF16),
             pltpu.VMEM((NCH, 8, B, HD), F32), pltpu.VMEM((NCH, 4, B, HD), F32),
             pltpu.VMEM((NCH, 4, B, HD), F32), pltpu.VMEM((NCH, 4, B, HD), F32),

time: 73 us -> 78 us (1.068)
  Pallas kernels: 71.5 us -> 76.5 us
    pallas_call x1, Pallas kernels: 49.4 us -> 54.4 us  [layer_step(): pl.pallas_call(tail_kernel, out_shape=pltpu.VMEM((B, D), BF16), in_specs=...]
where the time goes in v3:
time: 78 us; the launch traced here: 77.9 us
  Pallas kernels  76.5 us (98%)
    pallas_call x1, Pallas kernels, layer_step(): pl.pallas_call(tail_kernel, out_shape=pltpu.VMEM((B, D), BF16), in_specs=...  54.4 us
    pallas_call x1, Pallas kernels, layer_step(): pl.pallas_call(qkv_kernel, out_shape=(pltpu.VMEM((B * ROWS, HD), F32), pl...  12.5 us
    pallas_call x1, Pallas kernels, layer_step(): pl.pallas_call(attn_kernel, out_shape=(pltpu.VMEM((KVL, GRP + 1, B, HD),...  9.64 us

profile of v3, /device:TPU:0, one launch (start us, length us, event | category | flops | bytes accessed | tf_op | source)
XLA Modules:
  0.0 77.9 jit_solution(12486108729194500151)
XLA Ops:
  0.6 12.5 %qkv.1 = (f32[768,128]{1,0:T(8,128)S(1)}, f32[256,128]{1,0:T(8,128)S(1)}, f32[256,128]{1,0:T(8,128)S(1)}, bf16[32,1024,128]{2,1,0:T(8,128)(2,1)S(1)}, bf16[32,1024,128]{2,1,0:T(8,128)(2,1)S(1)}) custom-call(s32[32]{0:T(128)} %ctx_ref.3, f32[1,128]{1,0:T(1,128)} %constant.2.clone.freq_ref, bf16[32,5120]{1,0:T(8,128)(2,1)} %x_hbm.3, bf16[40,128]{1,0:T(8,128)(2,1)} %bitcast.13, ...), custom_call_target="tpu_custom_call" | custom-call | tf_op jit(solution)/shard_map/qkv/pallas_call | solution.py:441
  13.1 9.6 %attn.1 = (f32[4,6,32,128]{3,2,1,0:T(8,128)S(1)}, bf16[32,1024,128]{2,1,0:T(8,128)(2,1)S(1)}, bf16[32,1024,128]{2,1,0:T(8,128)(2,1)S(1)}, bf16[32,1024,128]{2,1,0:T(8,128)(2,1)}, bf16[32,1024,128]{2,1,0:T(8,128)(2,1)}) custom-call(s32[32]{0:T(128)} %ctx_ref.3, f32[768,128]{1,0:T(8,128)S(1)} %get-tuple-element.11.q_ref, ...), custom_call_target="tpu_custom_call", output_to_operand_aliasing={{1}: (4, {}), {2}: (5, {})} | custom-call | tf_op jit(solution)/shard_map/attn/pallas_call | solution.py:456
  22.8 54.4 %tail.1 = bf16[32,5120]{1,0:T(8,128)(2,1)S(1)} custom-call(f32[4,6,32,128]{3,2,1,0:T(8,128)S(1)} %get-tuple-element.16.part_ref, bf16[32,5120]{1,0:T(8,128)(2,1)} %x_hbm.3, bf16[40,128]{1,0:T(8,128)(2,1)} %bitcast.12, bf16[640,5120]{1,0:T(8,128)(2,1)} %wo_hbm.1, bf16[1728,5120]{1,0:T(8,128)(2,1)} %bitcast.8, bf16[1728,5120]{1,0:T(8,128)(2,1)} %bitcast.9, ...), custom_call_target="tpu_custom_call" | custom-call | flops 10000000000 | bytes 100000000 | tf_op jit(solution)/shard_map/tail/pallas_call | solution.py:472
  77.1 0.7 copy.20

commit v4 on v3

--- a/solution.py
+++ b/solution.py
@@ -216,7 +216,8 @@
 CW = D // NCH
 GCH = 256
 FLIP = 4
-FLIPS = (4, 1, 3, 3, 1)
+AHEAD = 3
+FLIPS = (3, 1, 3, 3, 2)
 
 
 def tail_kernel(part_ref, x_hbm, g_hbm, wo_hbm, wg_hbm, wu_hbm, wd_hbm, out_ref,
@@ -265,9 +266,9 @@
     wo_copy.wait()
     x_copy.wait()
     g_copy.wait()
-    for i in range(len(spans)):
-        gate_copy(i, 0).start()
-        gate_copy(i, 1).start()
+    order = [(i, which) for i in range(len(spans)) for which in range(2)]
+    for block in range(AHEAD):
+        gate_copy(*order[block]).start()
 
     flipped = [0]
 
@@ -275,6 +276,8 @@
         for block in range(flipped[0], min(flipped[0] + blocks, 2 * full)):
             i, which = block // 2, block % 2
             gate_copy(i, which).wait()
+            if block + AHEAD < len(order):
+                gate_copy(*order[block + AHEAD]).start()
 
             @pl.loop(0, D // (GCH * FLIP))
             def _(u):

time: 78 us -> 78 us (level)
  no operation moved by 1% of the time
where the time goes in v4:
time: 78 us; the launch traced here: 77.9 us
  Pallas kernels  76.5 us (98%)
    pallas_call x1, Pallas kernels, layer_step(): pl.pallas_call(tail_kernel, out_shape=pltpu.VMEM((B, D), BF16), in_specs=...  54.4 us
    pallas_call x1, Pallas kernels, layer_step(): pl.pallas_call(qkv_kernel, out_shape=(pltpu.VMEM((B * ROWS, HD), F32), pl...  12.5 us
    pallas_call x1, Pallas kernels, layer_step(): pl.pallas_call(attn_kernel, out_shape=(pltpu.VMEM((KVL, GRP + 1, B, HD),...  9.64 us

profile of v4, /device:TPU:0, one launch (start us, length us, event | category | flops | bytes accessed | tf_op | source)
XLA Modules:
  0.0 77.9 jit_solution(9917589122161164674)
XLA Ops:
  0.6 12.5 %qkv.1 = (f32[768,128]{1,0:T(8,128)S(1)}, f32[256,128]{1,0:T(8,128)S(1)}, f32[256,128]{1,0:T(8,128)S(1)}, bf16[32,1024,128]{2,1,0:T(8,128)(2,1)S(1)}, bf16[32,1024,128]{2,1,0:T(8,128)(2,1)S(1)}) custom-call(s32[32]{0:T(128)} %ctx_ref.3, f32[1,128]{1,0:T(1,128)} %constant.2.clone.freq_ref, bf16[32,5120]{1,0:T(8,128)(2,1)} %x_hbm.3, bf16[40,128]{1,0:T(8,128)(2,1)} %bitcast.13, ...), custom_call_target="tpu_custom_call" | custom-call | tf_op jit(solution)/shard_map/qkv/pallas_call | solution.py:444
  13.1 9.6 %attn.1 = (f32[4,6,32,128]{3,2,1,0:T(8,128)S(1)}, bf16[32,1024,128]{2,1,0:T(8,128)(2,1)S(1)}, bf16[32,1024,128]{2,1,0:T(8,128)(2,1)S(1)}, bf16[32,1024,128]{2,1,0:T(8,128)(2,1)}, bf16[32,1024,128]{2,1,0:T(8,128)(2,1)}) custom-call(s32[32]{0:T(128)} %ctx_ref.3, f32[768,128]{1,0:T(8,128)S(1)} %get-tuple-element.11.q_ref, ...), custom_call_target="tpu_custom_call", output_to_operand_aliasing={{1}: (4, {}), {2}: (5, {})} | custom-call | tf_op jit(solution)/shard_map/attn/pallas_call | solution.py:459
  22.8 54.4 %tail.1 = bf16[32,5120]{1,0:T(8,128)(2,1)S(1)} custom-call(f32[4,6,32,128]{3,2,1,0:T(8,128)S(1)} %get-tuple-element.16.part_ref, bf16[32,5120]{1,0:T(8,128)(2,1)} %x_hbm.3, bf16[40,128]{1,0:T(8,128)(2,1)} %bitcast.12, bf16[640,5120]{1,0:T(8,128)(2,1)} %wo_hbm.1, bf16[1728,5120]{1,0:T(8,128)(2,1)} %bitcast.8, bf16[1728,5120]{1,0:T(8,128)(2,1)} %bitcast.9, ...), custom_call_target="tpu_custom_call" | custom-call | flops 10000000000 | bytes 100000000 | tf_op jit(solution)/shard_map/tail/pallas_call | solution.py:475
  77.2 0.7 copy.20

commit v5 on v2

--- a/solution.py
+++ b/solution.py
@@ -37,11 +37,14 @@
     pl.semaphore_wait(barrier, len(peers))
 
 
+WPARTS = 4
+CPARTS = 8
+FLIGHT = 6
 CHUNKS = ((0, 2), (2, 2), (4, 2), (6, 1))
 
 
 def qkv_kernel(ctx_ref, freq_ref, x_hbm, g_hbm, w_ref, k_hbm, v_hbm, q_ref, kn_ref, vn_ref, kc_ref, vc_ref,
-               x_ref, g_ref, wbuf, u_ref, ex, x_sem, w_sem, c_sem, m_send, m_recv, x_send, x_recv, r_send, r_recv):
+               x_ref, g_ref, wbuf, u_ref, ex, x_sem, w_sem, m_send, m_recv, x_send, x_recv, r_send, r_recv):
     j = lax.axis_index("kvp")
     mate = {"kvp": j + 1 - 2 * lax.rem(j, 2)}
     side = {"kvp": lax.rem(j + 2, 4)}
@@ -50,18 +53,26 @@
     x_copy.start()
     g_copy.start()
 
-    def cache_copy(i):
-        src, dst = ((k_hbm, kc_ref), (v_hbm, vc_ref))[i // 4]
-        some = pl.ds((i % 4) * 8, 8)
-        return pltpu.make_async_copy(src.at[some], dst.at[some], c_sem.at[i])
-
-    def load(i):
-        first, n = CHUNKS[i]
-        cols = pl.ds(pl.multiple_of(j * QCOLS + first * HD, HD), n * HD)
-        return pltpu.make_async_copy(w_ref.at[:, cols], wbuf.at[:, pl.ds(first * HD, n * HD)], w_sem.at[i])
-
-    load(0).start()
-    load(1).start()
+    pieces = []
+    last_piece = []
+    for first, n in CHUNKS:
+        depth = D * 2 // (WPARTS * n)
+        for part in range(D // depth):
+            rows = pl.ds(part * depth, depth)
+            cols = pl.ds(pl.multiple_of(j * QCOLS + first * HD, HD), n * HD)
+            pieces.append((w_ref.at[rows, cols], wbuf.at[rows, pl.ds(first * HD, n * HD)]))
+        last_piece.append(len(pieces))
+    n_weight = len(pieces)
+    for i in range(2 * CPARTS):
+        src, dst = ((k_hbm, kc_ref), (v_hbm, vc_ref))[i // CPARTS]
+        some = pl.ds((i % CPARTS) * (B // CPARTS), B // CPARTS)
+        pieces.append((src.at[some], dst.at[some]))
+
+    def fetch(i):
+        return pltpu.make_async_copy(*pieces[i], w_sem.at[i])
+
+    for i in range(FLIGHT):
+        fetch(i).start()
     enter((mate, side))
     row = lax.broadcasted_iota(jnp.int32, (B, HD), 0)
     lane = lax.broadcasted_iota(jnp.int32, (B, HD), 1)
@@ -99,12 +110,12 @@
         return remote(piece(slot, i), piece(slot, i), r_send.at[i], r_recv.at[i], mate)
 
     for i, (first, n) in enumerate(CHUNKS):
-        load(i).wait()
-        if i + 2 < len(CHUNKS):
-            load(i + 2).start()
-        else:
-            for c in range((i - 2) * 4, (i - 1) * 4):
-                cache_copy(c).start()
+        for p in range(last_piece[i - 1] if i else 0, last_piece[i]):
+            fetch(p).wait()
+            fetch(p + FLIGHT).start()
+        if i == len(CHUNKS) - 1:
+            for p in range(n_weight + FLIGHT, len(pieces)):
+                fetch(p).start()
         res = jnp.dot(u_ref[...], wbuf[:, first * HD:(first + n) * HD], preferred_element_type=F32)
         for h in range(n):
             tile = res[:, h * HD:(h + 1) * HD]
@@ -131,8 +142,8 @@
         to_side(i).wait_send()
         to_mate(i).wait_send()
         relay(i).wait_send()
-    for i in range(8):
-        cache_copy(i).wait()
+    for i in range(n_weight, len(pieces)):
+        fetch(i).wait()
 
 
 PAIRS = B // 2
@@ -156,15 +167,14 @@
 
     def patch(b):
         pos = ctx_ref[b] - base
-
-        @pl.when((pos >= 0) & (pos < T))
-        def _():
-            win = pl.ds(pl.multiple_of((pos // 4) * 16, 16), 16)
-            hit = (wrow // KVL) == (pos & 3)
-            for new_ref, buf in ((kn_ref, kbuf), (vn_ref, vbuf)):
-                new8 = new_ref[pl.ds(b * 8, 8), :]
-                new16 = jnp.concatenate([new8, new8], axis=0)
-                buf[b, win, :] = jnp.where(hit, new16, buf[b, win, :].astype(F32)).astype(BF16)
+        here = (pos >= 0) & (pos < T)
+        pos = jnp.clip(pos, 0, T - 1)
+        win = pl.ds(pl.multiple_of((pos // 4) * 16, 16), 16)
+        hit = (wrow // KVL) == jnp.where(here, pos & 3, 4)
+        for new_ref, buf in ((kn_ref, kbuf), (vn_ref, vbuf)):
+            new8 = new_ref[pl.ds(b * 8, 8), :]
+            new16 = jnp.concatenate([new8, new8], axis=0)
+            buf[b, win, :] = jnp.where(hit, new16, buf[b, win, :].astype(F32)).astype(BF16)
 
     def attend(p):
         b = 2 * p
@@ -191,10 +201,10 @@
         flush(it, 0).start()
         flush(it, 1).start()
 
-    @pl.loop(0, PAIRS // 2)
+    @pl.loop(0, PAIRS // 4)
     def _(it):
-        for k in range(2):
-            attend(it * 2 + k)
+        for k in range(4):
+            attend(it * 4 + k)
 
     lane = lax.broadcasted_iota(jnp.int32, (B, HD), 1)
     for g in range(KVL):
@@ -410,7 +420,7 @@
         scratch_shapes=[
             pltpu.VMEM((B, D), BF16), pltpu.VMEM((D // HD, HD), BF16),
             pltpu.VMEM((D, QCOLS), BF16), pltpu.VMEM((B, D), BF16), pltpu.VMEM((KVL, GRP + 2, B, HD), F32),
-            dma(2), dma(nch), dma(8), dma(nch), dma(nch), dma(nch), dma(nch), dma(nch), dma(nch),
+            dma(2), dma(4 * WPARTS + 2 * CPARTS), dma(nch), dma(nch), dma(nch), dma(nch), dma(nch), dma(nch),
         ],
         compiler_params=pltpu.CompilerParams(collective_id=0, has_side_effects=True, vmem_limit_bytes=MIB * 16),
         name="qkv",

time: 73 us -> 72.6 us (level)
    pallas_call x1, Pallas kernels: 9.64 us -> 8.73 us  [layer_step(): pl.pallas_call(attn_kernel, out_shape=(pltpu.VMEM((KVL, GRP + 1, B, HD),...]
where the time goes in v5:
time: 72.6 us; the launch traced here: 72.4 us
  Pallas kernels  71 us (98%)
  local copies, waits for them, and re-layouts  0.73 us (1%)
    pallas_call x1, Pallas kernels, layer_step(): pl.pallas_call(tail_kernel, out_shape=pltpu.VMEM((B, D), BF16), in_specs=...  49.3 us
    pallas_call x1, Pallas kernels, layer_step(): pl.pallas_call(qkv_kernel, out_shape=(pltpu.VMEM((B * ROWS, HD), F32), pl...  13 us
    pallas_call x1, Pallas kernels, layer_step(): pl.pallas_call(attn_kernel, out_shape=(pltpu.VMEM((KVL, GRP + 1, B, HD),...  8.73 us

profile of v5, /device:TPU:0, one launch (start us, length us, event | category | flops | bytes accessed | tf_op | source)
XLA Modules:
  0.0 72.4 jit_solution(879325905603411527)
XLA Ops:
  0.6 13.0 %qkv.1 = (f32[768,128]{1,0:T(8,128)S(1)}, f32[256,128]{1,0:T(8,128)S(1)}, f32[256,128]{1,0:T(8,128)S(1)}, bf16[32,1024,128]{2,1,0:T(8,128)(2,1)S(1)}, bf16[32,1024,128]{2,1,0:T(8,128)(2,1)S(1)}) custom-call(s32[32]{0:T(128)} %ctx_ref.3, f32[1,128]{1,0:T(1,128)} %constant.2.clone.freq_ref, bf16[32,5120]{1,0:T(8,128)(2,1)} %x_hbm.3, bf16[40,128]{1,0:T(8,128)(2,1)} %bitcast.13, ...), custom_call_target="tpu_custom_call" | custom-call | tf_op jit(solution)/shard_map/qkv/pallas_call | solution.py:414
  13.7 8.7 %attn.1 = (f32[4,6,32,128]{3,2,1,0:T(8,128)S(1)}, bf16[32,1024,128]{2,1,0:T(8,128)(2,1)S(1)}, bf16[32,1024,128]{2,1,0:T(8,128)(2,1)S(1)}, bf16[32,1024,128]{2,1,0:T(8,128)(2,1)}, bf16[32,1024,128]{2,1,0:T(8,128)(2,1)}) custom-call(s32[32]{0:T(128)} %ctx_ref.3, f32[768,128]{1,0:T(8,128)S(1)} %get-tuple-element.11.q_ref, ...), custom_call_target="tpu_custom_call", output_to_operand_aliasing={{1}: (4, {}), {2}: (5, {})} | custom-call | tf_op jit(solution)/shard_map/attn/pallas_call | solution.py:429
  22.4 49.3 %tail.1 = bf16[32,5120]{1,0:T(8,128)(2,1)S(1)} custom-call(f32[4,6,32,128]{3,2,1,0:T(8,128)S(1)} %get-tuple-element.16.part_ref, bf16[32,5120]{1,0:T(8,128)(2,1)} %x_hbm.3, bf16[40,128]{1,0:T(8,128)(2,1)} %bitcast.12, bf16[640,5120]{1,0:T(8,128)(2,1)} %wo_hbm.1, bf16[1728,5120]{1,0:T(8,128)(2,1)} %bitcast.8, bf16[1728,5120]{1,0:T(8,128)(2,1)} %bitcast.9, ...), custom_call_target="tpu_custom_call" | custom-call | flops 10000000000 | bytes 100000000 | tf_op jit(solution)/shard_map/tail/pallas_call | solution.py:445
  71.7 0.7 %copy.20 = bf16[32,5120]{1,0:T(8,128)(2,1)} copy(bf16[32,5120]{1,0:T(8,128)(2,1)S(1)} %tail.1) | data formatting | bytes 655360

commit v6 on v5

--- a/solution.py
+++ b/solution.py
@@ -66,7 +66,7 @@
     for i in range(2 * CPARTS):
         src, dst = ((k_hbm, kc_ref), (v_hbm, vc_ref))[i // CPARTS]
         some = pl.ds((i % CPARTS) * (B // CPARTS), B // CPARTS)
-        pieces.append((src.at[some], dst.at[some]))
+        pieces.append((src.at[some], dst.at[some, pl.ds(0, KVL * T)]))
 
     def fetch(i):
         return pltpu.make_async_copy(*pieces[i], w_sem.at[i])
@@ -147,6 +147,7 @@
 
 
 PAIRS = B // 2
+CPITCH = KVL * T + 16
 
 
 def attn_kernel(ctx_ref, q_ref, kn_ref, vn_ref, k_ref, v_ref, part_ref, kbuf, vbuf, ko_ref, vo_ref, bias, acc2, m2, l2, out_sem):
@@ -155,7 +156,7 @@
     def flush(i, which):
         src, dst = ((kbuf, ko_ref), (vbuf, vo_ref))[which]
         some = pl.ds(4 * i, 4)
-        return pltpu.make_async_copy(src.at[some], dst.at[some], out_sem.at[which, i])
+        return pltpu.make_async_copy(src.at[some, pl.ds(0, KVL * T)], dst.at[some], out_sem.at[which, i])
 
     row = lax.broadcasted_iota(jnp.int32, (2 * ROWS, KVL * T), 0)
     row = jnp.where(row >= ROWS, row - ROWS, row)
@@ -180,14 +181,14 @@
         b = 2 * p
         q = q_ref[pl.ds(p * 2 * ROWS, 2 * ROWS), :]
         lhs = jnp.concatenate([jnp.where(first_half, q, 0.0), jnp.where(first_half, 0.0, q)], axis=1).astype(BF16)
-        keys = jnp.concatenate([kbuf[b], kbuf[b + 1]], axis=1)
+        keys = jnp.concatenate([kbuf[b, :KVL * T], kbuf[b + 1, :KVL * T]], axis=1)
         s = lax.dot_general(lhs, keys, (((1,), (1,)), ((), ())), preferred_element_type=F32)
         lim = jnp.where(first_half, (ctx_ref[b] - base + 1) * KVL, (ctx_ref[b + 1] - base + 1) * KVL)
         cols = lax.broadcasted_iota(jnp.int32, (2 * ROWS, KVL * T), 1)
         s = jnp.where(cols < lim, s * HD ** -0.5 + bias[...], NEG_FILL)
         m = jnp.max(s, axis=1, keepdims=True)
         w = jnp.exp(s - m)
-        values = jnp.concatenate([vbuf[b], vbuf[b + 1]], axis=1)
+        values = jnp.concatenate([vbuf[b, :KVL * T], vbuf[b + 1, :KVL * T]], axis=1)
         o = jnp.dot(w.astype(BF16), values, preferred_element_type=F32)
         rows = pl.ds(p * 2 * ROWS, 2 * ROWS)
         acc2[rows, :] = jnp.where(first_half, o[:, :HD], o[:, HD:])
@@ -225,10 +226,13 @@
 NCH = 5
 CW = D // NCH
 GCH = 256
+FLIP = 4
+AHEAD = 3
+FLIPS = (4, 1, 3, 3, 1)
 
 
 def tail_kernel(part_ref, x_hbm, g_hbm, wo_hbm, wg_hbm, wu_hbm, wd_hbm, out_ref,
-                x_ref, g_ref, wo, wg, wu, rx, attn, n_ref, y_ref, pbuf, sbuf, pair_a, pair_b, rs_a, rs_b, ag_a, ag_b,
+                x_ref, g_ref, wo, w2, rx, attn, n_ref, y_ref, pbuf, sbuf, pair_a, pair_b, rs_a, rs_b, ag_a, ag_b,
                 x_sem, w_sem, gu_sem, wd_sem, c_send, c_recv, d_send, d_recv, s_send, s_recv, a_send, a_recv, f_send, f_recv):
     t = lax.axis_index("tp")
     j = lax.axis_index("kvp")
@@ -243,8 +247,21 @@
         chips.append(({"tp": tt, "kvp": xx * 2 + core}, tt * 2 + xx))
     ring = [{"tp": t, "kvp": lax.rem(j + d, 4)} for d in (1, 2, 3)]
 
+    full = FFL // GCH
+    rest = FFL - full * GCH
+    spans = [(i * GCH, GCH) for i in range(full)] + [(full * GCH, rest)]
+
+    def gate_copy(i, which):
+        first, n = spans[i]
+        src = (wg_hbm, wu_hbm)[which]
+        return pltpu.make_async_copy(src.at[pl.ds(first, n)], w2.at[which, pl.ds(first, n), pl.ds(0, D)], gu_sem.at[which, i])
+
+    order = [(i, which) for i in range(len(spans)) for which in range(2)]
+    for block in range(AHEAD - 1):
+        gate_copy(*order[block]).start()
     wo_copy = pltpu.make_async_copy(wo_hbm, wo, w_sem)
     wo_copy.start()
+    gate_copy(*order[AHEAD - 1]).start()
     x_copy = pltpu.make_async_copy(x_hbm, x_ref, x_sem.at[0])
     g_copy = pltpu.make_async_copy(g_hbm, g_ref, x_sem.at[1])
     x_copy.start()
@@ -257,26 +274,32 @@
     for d in (2, 1, 3):
         combine_copy(d).start()
 
-    full = FFL // GCH
-    rest = FFL - full * GCH
-    spans = [(i * GCH, GCH) for i in range(full)] + [(full * GCH, rest)]
-
-    def gate_copy(i, which):
-        first, n = spans[i]
-        src, dst = ((wg_hbm, wg), (wu_hbm, wu))[which]
-        return pltpu.make_async_copy(src.at[pl.ds(first, n)], dst.at[pl.ds(first, n)], gu_sem.at[which, i])
-
     def down_copy(i):
         rows = pl.ds(*spans[i])
-        return pltpu.make_async_copy(wd_hbm.at[rows], wg.at[rows], wd_sem.at[i])
-
+        return pltpu.make_async_copy(wd_hbm.at[rows], w2.at[0, rows, pl.ds(0, D)], wd_sem.at[i])
+
+
+    flipped = [0]
+
+    def flip(blocks):
+        for block in range(flipped[0], flipped[0] + blocks):
+            i, which = order[block]
+            gate_copy(i, which).wait()
+            if block + AHEAD < len(order):
+                gate_copy(*order[block + AHEAD]).start()
+
+            @pl.loop(0, D // (GCH * FLIP))
+            def _(u):
+                for v in range(FLIP):
+                    rows = pl.ds(i * GCH, GCH)
+                    cols = pl.ds(pl.multiple_of((u * FLIP + v) * GCH, GCH), GCH)
+                    w2[which, rows, cols] = w2[which, rows, cols].T
+        flipped[0] += blocks
+
+    flip(FLIPS[0])
     wo_copy.wait()
     x_copy.wait()
     g_copy.wait()
-    for i in range(len(spans)):
-        gate_copy(i, 0).start()
-        gate_copy(i, 1).start()
-
     for d in (1, 2, 3):
         combine_copy(d).wait_recv()
     stats = [part_ref[j, GRP]] + [rx[i, GRP] for i in range(3)]
@@ -313,12 +336,16 @@
             for i in range(8):
                 pbuf[k, i] = res[:, i * HD:(i + 1) * HD]
             pair_copy(k).start()
+        if which == 0:
+            flip(FLIPS[1])
         for k in range(NCH):
             pair_copy(k).wait_recv()
             for i in range(4):
                 sbuf[k, i] = pbuf[k, core * 4 + i] + pair[k, i]
             for e in (2, 0, 1):
                 scatter_copy(k, e).start()
+        if which == 0:
+            flip(FLIPS[2])
         for k in range(NCH):
             for e in range(3):
                 scatter_copy(k, e).wait_recv()
@@ -326,10 +353,16 @@
             ag[k * 8 + own] = (base(k * 8 + own) + total).astype(BF16).astype(F32)
             for e in (2, 0, 1, 3):
                 gather_copy(k, e).start()
+        if which == 0:
+            flip(FLIPS[3])
         for k in range(NCH):
             for e in range(3):
                 gather_copy(k, e).wait_recv()
                 forward_copy(k, e).start()
+        if which == 0:
+            flip(FLIPS[4])
+            for block in range(sum(FLIPS) + AHEAD, len(order)):
+                gate_copy(*order[block]).start()
         for k in range(NCH):
             gather_copy(k, 3).wait_recv()
             for e in range(3):
@@ -357,22 +390,28 @@
     for i in range(D // HD):
         n_ref[:, i * HD:(i + 1) * HD] = (ag_a[i] * inv * g_ref[i:i + 1, :].astype(F32)).astype(BF16)
 
-    def gate_step(first, n):
-        dims = (((1,), (1,)), ((), ()))
-        gate = lax.dot_general(n_ref[...], wg[pl.ds(first, n), :], dims, preferred_element_type=F32)
-        up = lax.dot_general(n_ref[...], wu[pl.ds(first, n), :], dims, preferred_element_type=F32)
+    def act(gate, up):
         return (jax.nn.silu(gate) * up).astype(BF16)
 
     for i, (first, n) in enumerate(spans):
-        gate_copy(i, 0).wait()
-        gate_copy(i, 1).wait()
-        y_ref[:, first:first + n] = gate_step(first, n)
+        rows = pl.ds(first, n)
+        for which in range(2):
+            if 2 * i + which >= sum(FLIPS):
+                gate_copy(i, which).wait()
+        sums = [None, None]
+        for k in range(D // GCH):
+            cols = slice(k * GCH, (k + 1) * GCH)
+            for which in range(2):
+                dims = (((1,), (0 if 2 * i + which < sum(FLIPS) else 1,)), ((), ()))
+                term = lax.dot_general(n_ref[:, cols], w2[which, rows, cols], dims, preferred_element_type=F32)
+                sums[which] = term if k == 0 else sums[which] + term
+        y_ref[:, first:first + n] = act(sums[0], sums[1])
         down_copy(i).start()
     for i in range(len(spans)):
         down_copy(i).wait()
 
     def down_product(k):
-        return jnp.dot(y_ref[...], wg[:, k * CW:(k + 1) * CW], preferred_element_type=F32)
+        return jnp.dot(y_ref[...], w2[0, :, k * CW:(k + 1) * CW], preferred_element_type=F32)
 
     all_sum(1, down_product, lambda i: ag_a[i], pair_b, rs_b, ag_b)
     for i in range(D // HD):
@@ -411,10 +450,10 @@
     kc = k_cache.reshape(B, T * KVL, HD)
     vc = v_cache.reshape(B, T * KVL, HD)
     nch = len(CHUNKS)
-    q2, kn, vn, kc, vc = pl.pallas_call(
+    q2, kn, vn, kv, vv = pl.pallas_call(
         qkv_kernel,
         out_shape=(pltpu.VMEM((B * ROWS, HD), F32), pltpu.VMEM((B * 8, HD), F32), pltpu.VMEM((B * 8, HD), F32),
-                   pltpu.VMEM(kc.shape, BF16), pltpu.VMEM(vc.shape, BF16)),
+                   pltpu.VMEM((B, CPITCH, HD), BF16), pltpu.VMEM((B, CPITCH, HD), BF16)),
         in_specs=[smem(), vmem(), hbm(), hbm(), hbm(), hbm(), hbm()],
         out_specs=(vmem(),) * 5,
         scratch_shapes=[
@@ -426,9 +465,9 @@
         name="qkv",
     )(in_hbm(ctx_len), in_hbm(freq), in_hbm(x_in), in_hbm(g_attn.reshape(D // HD, HD)), in_hbm(w_qkv), in_hbm(kc), in_hbm(vc))
 
-    part, kc, vc, k_out, v_out = pl.pallas_call(
+    part, _, _, k_out, v_out = pl.pallas_call(
         attn_kernel,
-        out_shape=(pltpu.VMEM((KVL, GRP + 1, B, HD), F32), pltpu.VMEM(kc.shape, BF16), pltpu.VMEM(vc.shape, BF16),
+        out_shape=(pltpu.VMEM((KVL, GRP + 1, B, HD), F32), pltpu.VMEM((B, CPITCH, HD), BF16), pltpu.VMEM((B, CPITCH, HD), BF16),
                    jax.ShapeDtypeStruct(kc.shape, BF16), jax.ShapeDtypeStruct(vc.shape, BF16)),
         in_specs=[smem(), vmem(), vmem(), vmem(), vmem(), vmem()],
         out_specs=(vmem(), vmem(), vmem(), hbm(), hbm()),
@@ -440,7 +479,7 @@
         input_output_aliases={4: 1, 5: 2},
         compiler_params=pltpu.CompilerParams(vmem_limit_bytes=MIB * 4),
         name="attn",
-    )(in_hbm(ctx_len), q2, kn, vn, kc, vc)
+    )(in_hbm(ctx_len), q2, kn, vn, kv, vv)
 
     x_out = pl.pallas_call(
         tail_kernel,
@@ -448,7 +487,7 @@
         in_specs=[vmem(), hbm(), hbm(), hbm(), hbm(), hbm(), hbm()],
         out_specs=vmem(),
         scratch_shapes=[
-            pltpu.VMEM((B, D), BF16), pltpu.VMEM((D // HD, HD), BF16), pltpu.VMEM(w_o.shape, BF16), pltpu.VMEM((FFL, D), BF16), pltpu.VMEM((FFL, D), BF16),
+            pltpu.VMEM((B, D), BF16), pltpu.VMEM((D // HD, HD), BF16), pltpu.VMEM(w_o.shape, BF16), pltpu.VMEM((2, FFL, D + HD), BF16),
             pltpu.VMEM((3, GRP + 1, B, HD), F32), pltpu.VMEM((B, GRP * HD), BF16), pltpu.VMEM((B, D), BF16), pltpu.VMEM((B, FFL), BF16),
             pltpu.VMEM((NCH, 8, B, HD), F32), pltpu.VMEM((NCH, 4, B, HD), F32),
             pltpu.VMEM((NCH, 4, B, HD), F32), pltpu.VMEM((NCH, 4, B, HD), F32),

time: 72.6 us -> 74.2 us (1.022)
  Pallas kernels: 71 us -> 72.7 us
    pallas_call x1, Pallas kernels: 49.3 us -> 50.9 us  [layer_step(): pl.pallas_call(tail_kernel, out_shape=pltpu.VMEM((B, D), BF16), in_specs=...]
where the time goes in v6:
time: 74.2 us; the launch traced here: 74.1 us
  Pallas kernels  72.7 us (98%)
    pallas_call x1, Pallas kernels, layer_step(): pl.pallas_call(tail_kernel, out_shape=pltpu.VMEM((B, D), BF16), in_specs=...  50.9 us
    pallas_call x1, Pallas kernels, layer_step(): pl.pallas_call(qkv_kernel, out_shape=(pltpu.VMEM((B * ROWS, HD), F32), pl...  13 us
    pallas_call x1, Pallas kernels, layer_step(): pl.pallas_call(attn_kernel, out_shape=(pltpu.VMEM((KVL, GRP + 1, B, HD),...  8.73 us

profile of v6, /device:TPU:0, one launch (start us, length us, event | category | flops | bytes accessed | tf_op | source)
XLA Modules:
  0.0 74.1 jit_solution(10843148951784869070)
XLA Ops:
  0.6 13.0 %qkv.1 = (f32[768,128]{1,0:T(8,128)S(1)}, f32[256,128]{1,0:T(8,128)S(1)}, f32[256,128]{1,0:T(8,128)S(1)}, bf16[32,1040,128]{2,1,0:T(8,128)(2,1)S(1)}, bf16[32,1040,128]{2,1,0:T(8,128)(2,1)S(1)}) custom-call(s32[32]{0:T(128)} %ctx_ref.3, f32[1,128]{1,0:T(1,128)} %constant.2.clone.freq_ref, bf16[32,5120]{1,0:T(8,128)(2,1)} %x_hbm.3, bf16[40,128]{1,0:T(8,128)(2,1)} %bitcast.13, ...), custom_call_target="tpu_custom_call" | custom-call | tf_op jit(solution)/shard_map/qkv/pallas_call | solution.py:453
  13.7 8.7 %attn.1 = (f32[4,6,32,128]{3,2,1,0:T(8,128)S(1)}, bf16[32,1040,128]{2,1,0:T(8,128)(2,1)S(1)}, bf16[32,1040,128]{2,1,0:T(8,128)(2,1)S(1)}, bf16[32,1024,128]{2,1,0:T(8,128)(2,1)}, bf16[32,1024,128]{2,1,0:T(8,128)(2,1)}) custom-call(s32[32]{0:T(128)} %ctx_ref.3, f32[768,128]{1,0:T(8,128)S(1)} %get-tuple-element.11.q_ref, ...), custom_call_target="tpu_custom_call", output_to_operand_aliasing={{1}: (4, {}), {2}: (5, {})} | custom-call | tf_op jit(solution)/shard_map/attn/pallas_call | solution.py:468
  22.4 50.9 %tail.1 = bf16[32,5120]{1,0:T(8,128)(2,1)S(1)} custom-call(f32[4,6,32,128]{3,2,1,0:T(8,128)S(1)} %get-tuple-element.16.part_ref, bf16[32,5120]{1,0:T(8,128)(2,1)} %x_hbm.3, bf16[40,128]{1,0:T(8,128)(2,1)} %bitcast.12, bf16[640,5120]{1,0:T(8,128)(2,1)} %wo_hbm.1, bf16[1728,5120]{1,0:T(8,128)(2,1)} %bitcast.8, bf16[1728,5120]{1,0:T(8,128)(2,1)} %bitcast.9, ...), custom_call_target="tpu_custom_call" | custom-call | flops 10000000000 | bytes 100000000 | tf_op jit(solution)/shard_map/tail/pallas_call | solution.py:484
  73.4 0.7 copy.20

commit v7 on v6

--- a/solution.py
+++ b/solution.py
@@ -228,7 +228,7 @@
 GCH = 256
 FLIP = 4
 AHEAD = 3
-FLIPS = (4, 1, 3, 3, 1)
+FLIPS = (2, 0, 2, 2, 0)
 
 
 def tail_kernel(part_ref, x_hbm, g_hbm, wo_hbm, wg_hbm, wu_hbm, wd_hbm, out_ref,

time: 74.2 us -> 71.1 us (0.958)
  Pallas kernels: 72.7 us -> 69.5 us
    pallas_call x1, Pallas kernels: 50.9 us -> 47.8 us  [layer_step(): pl.pallas_call(tail_kernel, out_shape=pltpu.VMEM((B, D), BF16), in_specs=...]
where the time goes in v7:
time: 71.1 us; the launch traced here: 70.9 us
  Pallas kernels  69.5 us (98%)
  local copies, waits for them, and re-layouts  0.73 us (1%)
    pallas_call x1, Pallas kernels, layer_step(): pl.pallas_call(tail_kernel, out_shape=pltpu.VMEM((B, D), BF16), in_specs=...  47.8 us
    pallas_call x1, Pallas kernels, layer_step(): pl.pallas_call(qkv_kernel, out_shape=(pltpu.VMEM((B * ROWS, HD), F32), pl...  13 us
    pallas_call x1, Pallas kernels, layer_step(): pl.pallas_call(attn_kernel, out_shape=(pltpu.VMEM((KVL, GRP + 1, B, HD),...  8.73 us

profile of v7, /device:TPU:0, one launch (start us, length us, event | category | flops | bytes accessed | tf_op | source)
XLA Modules:
  0.0 70.9 jit_solution(11015353484206851668)
XLA Ops:
  0.6 13.0 %qkv.1 = (f32[768,128]{1,0:T(8,128)S(1)}, f32[256,128]{1,0:T(8,128)S(1)}, f32[256,128]{1,0:T(8,128)S(1)}, bf16[32,1040,128]{2,1,0:T(8,128)(2,1)S(1)}, bf16[32,1040,128]{2,1,0:T(8,128)(2,1)S(1)}) custom-call(s32[32]{0:T(128)} %ctx_ref.3, f32[1,128]{1,0:T(1,128)} %constant.2.clone.freq_ref, bf16[32,5120]{1,0:T(8,128)(2,1)} %x_hbm.3, bf16[40,128]{1,0:T(8,128)(2,1)} %bitcast.13, ...), custom_call_target="tpu_custom_call" | custom-call | tf_op jit(solution)/shard_map/qkv/pallas_call | solution.py:453
  13.7 8.7 %attn.1 = (f32[4,6,32,128]{3,2,1,0:T(8,128)S(1)}, bf16[32,1040,128]{2,1,0:T(8,128)(2,1)S(1)}, bf16[32,1040,128]{2,1,0:T(8,128)(2,1)S(1)}, bf16[32,1024,128]{2,1,0:T(8,128)(2,1)}, bf16[32,1024,128]{2,1,0:T(8,128)(2,1)}) custom-call(s32[32]{0:T(128)} %ctx_ref.3, f32[768,128]{1,0:T(8,128)S(1)} %get-tuple-element.11.q_ref, ...), custom_call_target="tpu_custom_call", output_to_operand_aliasing={{1}: (4, {}), {2}: (5, {})} | custom-call | tf_op jit(solution)/shard_map/attn/pallas_call | solution.py:468
  22.4 47.8 %tail.1 = bf16[32,5120]{1,0:T(8,128)(2,1)S(1)} custom-call(f32[4,6,32,128]{3,2,1,0:T(8,128)S(1)} %get-tuple-element.16.part_ref, bf16[32,5120]{1,0:T(8,128)(2,1)} %x_hbm.3, bf16[40,128]{1,0:T(8,128)(2,1)} %bitcast.12, bf16[640,5120]{1,0:T(8,128)(2,1)} %wo_hbm.1, bf16[1728,5120]{1,0:T(8,128)(2,1)} %bitcast.8, bf16[1728,5120]{1,0:T(8,128)(2,1)} %bitcast.9, ...), custom_call_target="tpu_custom_call" | custom-call | flops 10000000000 | bytes 100000000 | tf_op jit(solution)/shard_map/tail/pallas_call | solution.py:484
  70.2 0.7 %copy.20 = bf16[32,5120]{1,0:T(8,128)(2,1)} copy(bf16[32,5120]{1,0:T(8,128)(2,1)S(1)} %tail.1) | data formatting | bytes 655360
